TPU v7x, 128 devices: a whole 4x4x4 slice. The times are simulated.
128 devices in a mesh: bank: 4 (over y), zero: 32 (over z, x, core).
Axes of the slice: x: 4, y: 4, z: 4, core: 2. Of those that a mesh axis runs over, the one named last changes fastest.
Arguments:
- train_gate: float32 [64, 2048, 1024], P('bank', 'zero'), may hold values from -0.25 to 0.25
- train_up: float32 [64, 2048, 1024], P('bank', 'zero'), may hold values from -0.25 to 0.25
- train_down: float32 [64, 1024, 2048], P('bank', None, 'zero'), may hold values from -0.375 to 0.375
- router_weight: float32 [2048, 64], P('zero', 'bank'), may hold values from -0.125 to 0.125
- router_gain: float32 [2048], P('zero'), may hold values from 0.25 to 1.75
Outputs:
- ready_gate: bfloat16 [64, 2048, 1024], P('bank', None, 'zero')
- ready_up: bfloat16 [64, 2048, 1024], P('bank', None, 'zero')
- ready_down: bfloat16 [64, 1024, 2048], P('bank', 'zero')
- scale_gate: float32 [64, 1024], P('bank', 'zero')
- scale_up: float32 [64, 1024], P('bank', 'zero')
- scale_down: float32 [64, 1024], P('bank', 'zero')
- serve_router: bfloat16 [2048, 64], replicated
All inputs are finite; a program needn't handle non-finite values.
Results may differ from a plain program's by a relative error of at most 0.001.
Values may be sent and summed in bfloat16 or wider, within the bound.
A program may use at most 128 MiB of HBM per device.

v0:
```python
import jax
import jax.numpy as jnp
from jax import lax
from jax.sharding import Mesh
from jax.sharding import PartitionSpec as P

ZERO = ("zero_0", "zero_1", "zero_2")


def packed_total(arrays, axis):
    ends = [0]
    for a in arrays:
        ends.append(ends[-1] + a.size)
    total = lax.psum(jnp.concatenate([a.ravel() for a in arrays]), axis)
    return tuple(total[b:e].reshape(a.shape) for a, b, e in zip(arrays, ends, ends[1:]))


def laid_out(pieces, dim):
    lengths = list(pieces.shape[1:])
    lengths[dim] *= pieces.shape[0]
    return jnp.moveaxis(pieces, 0, dim).reshape(lengths)


def all_blocks(value, axes, turns):
    pieces = value[None]
    for k in turns:
        pieces = lax.all_gather(pieces, axes[k], axis=0, tiled=True)
    current = [lax.axis_size(axes[k]) for k in reversed(turns)]
    pieces = pieces.reshape(*current, *value.shape)
    turned = sorted(range(len(turns)), key=lambda place: turns[len(turns) - 1 - place])
    return pieces.transpose(*turned, *range(len(turns), pieces.ndim)).reshape(-1, *value.shape)


def gather_axes(value, axes, turns, dim):
    return laid_out(all_blocks(value, axes, turns), dim)


def body(train_gate, train_up, train_down, router_weight, router_gain):
    total_gate, total_up, total_down = packed_total(
        (
            jnp.sum(train_gate * train_gate, axis=1),
            jnp.sum(train_up * train_up, axis=1),
            jnp.sum(train_down * train_down, axis=2),
        ),
        ZERO,
    )
    scale_gate = jnp.sqrt(total_gate)
    scale_up = jnp.sqrt(total_up)
    scale_down = jnp.sqrt(total_down)
    narrow_gate, narrow_up, narrow_down = (
        (train_gate / jnp.expand_dims(scale_gate, 1)).astype(jnp.bfloat16),
        (train_up / jnp.expand_dims(scale_up, 1)).astype(jnp.bfloat16),
        (train_down / jnp.expand_dims(scale_down, 2)).astype(jnp.bfloat16),
    )
    ready_gate, ready_up = (
        lax.all_to_all(narrow_gate, ZERO, split_axis=2, concat_axis=1, tiled=True),
        lax.all_to_all(narrow_up, ZERO, split_axis=2, concat_axis=1, tiled=True),
    )
    ready_down = lax.all_to_all(narrow_down, ZERO, split_axis=1, concat_axis=2, tiled=True)
    scale_gate = lax.dynamic_slice_in_dim(
        scale_gate, lax.axis_index(ZERO) * ready_gate.shape[2], ready_gate.shape[2], axis=1
    )
    scale_up = lax.dynamic_slice_in_dim(
        scale_up, lax.axis_index(ZERO) * ready_up.shape[2], ready_up.shape[2], axis=1
    )
    scale_down = lax.dynamic_slice_in_dim(
        scale_down, lax.axis_index(ZERO) * ready_down.shape[1], ready_down.shape[1], axis=1
    )
    part_router = (router_weight * router_gain[:, None]).astype(jnp.bfloat16)
    row_router = gather_axes(part_router, (("zero_0", "zero_1"), "zero_2"), (0, 1), 0)
    serve_router = lax.all_gather(row_router, "bank", axis=1, tiled=True)
    return (ready_gate, ready_up, ready_down, scale_gate, scale_up, scale_down, serve_router)


def solution(mesh):
    split = Mesh(
        mesh.devices.reshape(mesh.shape["bank"], 4, 4, 2), ("bank", "zero_0", "zero_1", "zero_2")
    )
    placed = (
        P("bank", ZERO, None),
        P("bank", ZERO, None),
        P("bank", None, ZERO),
        P(ZERO, "bank"),
        P(ZERO),
    )
    return jax.shard_map(
        body,
        mesh=split,
        in_specs=placed,
        out_specs=(
            P("bank", None, ZERO),
            P("bank", None, ZERO),
            P("bank", ZERO, None),
            P("bank", ZERO),
            P("bank", ZERO),
            P("bank", ZERO),
            P(),
        ),
        check_vma=False,
    )
```

profile of v0, /device:TPU:1, one launch (start us, length us, event | category | flops | bytes accessed | tf_op | source)
XLA Modules:
  0.0 337.6 jit_solution(13221425438647020591)
XLA Ops:
  7.2 0.0 all-reduce.2.cloned.1.call-start
  7.2 0.0 copy-start
  7.2 0.0 copy-start.1
  7.2 3.0 multiply_reduce_fusion.2
  10.2 0.4 copy-done
  10.7 0.6 multiply_reduce_fusion.1
  11.3 0.6 copy-done.1
  11.9 0.6 multiply_reduce_fusion
  12.6 0.7 pad_maximum_fusion
  13.3 0.0 all-reduce.2.cloned.1.call-update
  13.3 8.1 %copy.28 = f32[16,64,1024]{1,0,2:T(8,128)} copy(f32[16,64,1024]{2,1,0:T(8,128)} %param.5) | data formatting | bytes 8388608 | tf_op args[0]
  21.4 98.1 %all-reduce.2.cloned.1.call-done = f32[49152]{0:T(1024)} async-done(((f32[49152]{0:T(1024)}), f32[49152]{0:T(1024)}) %all-reduce.2.cloned.1.call-update) | async-done | bytes 196624 | tf_op jit(solution)/shard_map/psum | solution.py:14
  119.5 1.0 slice_sqrt_fusion
  120.5 0.2 copy.27
  120.7 6.9 %fusion.1 = bf16[1024,16,64]{2,1,0:T(8,128)(2,1)} fusion(f32[16,64,1024]{1,0,2:T(8,128)} %copy.28, f32[16,1024]{0,1:T(8,128)S(1)} %copy.27), kind=kLoop, calls=%fused_computation.15 | loop fusion | flops 2097152 | bytes 6356992
  127.5 7.9 %reshape.68 = bf16[32,2,16384]{2,1,0:T(2,128)(2,1)} reshape(bf16[1024,16,64]{2,1,0:T(8,128)(2,1)} %fusion.1) | data formatting | bytes 4194304
  135.4 5.6 %all-to-all-start = ((bf16[32,2,16384]{2,1,0:T(2,128)(2,1)}), bf16[32,2,16384]{2,1,0:T(2,128)(2,1)S(1)}, u32[]{:S(2)}, u32[]{:S(2)}) async-start(bf16[32,2,16384]{2,1,0:T(2,128)(2,1)} %reshape.68), calls=%async_computation | async-start | bytes 4194304 | tf_op jit(solution)/shard_map/all_to_all | solution.py:56
  141.0 8.1 %copy.32 = f32[16,64,1024]{1,0,2:T(8,128)} copy(f32[16,64,1024]{2,1,0:T(8,128)} %param.6) | data formatting | bytes 8388608 | tf_op args[1]
  149.1 0.2 copy.31
  149.3 6.9 %fusion.2 = bf16[1024,16,64]{2,1,0:T(8,128)(2,1)} fusion(f32[16,64,1024]{1,0,2:T(8,128)} %copy.32, f32[16,1024]{0,1:T(8,128)S(1)} %copy.31), kind=kLoop, calls=%fused_computation.16 | loop fusion | flops 2097152 | bytes 6356992
  156.2 7.9 %reshape.70 = bf16[32,2,16384]{2,1,0:T(2,128)(2,1)} reshape(bf16[1024,16,64]{2,1,0:T(8,128)(2,1)} %fusion.2) | data formatting | bytes 4194304
  164.1 6.1 %all-to-all-done = bf16[32,2,16384]{2,1,0:T(2,128)(2,1)S(1)} async-done(((bf16[32,2,16384]{2,1,0:T(2,128)(2,1)}), bf16[32,2,16384]{2,1,0:T(2,128)(2,1)S(1)}, u32[]{:S(2)}, u32[]{:S(2)}) %all-to-all-start) | async-done | bytes 2097184 | tf_op jit(solution)/shard_map/all_to_all | solution.py:56
  170.1 5.2 %all-to-all-start.1 = ((bf16[32,2,16384]{2,1,0:T(2,128)(2,1)}), bf16[32,2,16384]{2,1,0:T(2,128)(2,1)}, u32[]{:S(2)}, u32[]{:S(2)}) async-start(bf16[32,2,16384]{2,1,0:T(2,128)(2,1)} %reshape.70), calls=%async_computation.1 | async-start | bytes 4194304 | tf_op jit(solution)/shard_map/all_to_all | solution.py:57
  175.4 8.1 %copy.36 = f32[16,1024,64]{2,0,1:T(8,128)} copy(f32[16,1024,64]{1,2,0:T(8,128)} %param.7) | data formatting | bytes 8388608 | tf_op args[2]
  183.5 0.2 copy.35
  183.7 6.9 %fusion.3 = bf16[1024,16,64]{2,1,0:T(8,128)(2,1)} fusion(f32[16,1024,64]{2,0,1:T(8,128)} %copy.36, f32[16,1024]{0,1:T(8,128)S(1)} %copy.35), kind=kLoop, calls=%fused_computation.17 | loop fusion | flops 2097152 | bytes 6356992
  190.5 0.0 copy-start.2
  190.5 0.0 copy-start.3
  190.5 7.9 %reshape.72 = bf16[32,2,16384]{2,1,0:T(2,128)(2,1)} reshape(bf16[1024,16,64]{2,1,0:T(8,128)(2,1)} %fusion.3) | data formatting | bytes 4194304
  198.4 5.8 %all-to-all-done.1 = bf16[32,2,16384]{2,1,0:T(2,128)(2,1)} async-done(((bf16[32,2,16384]{2,1,0:T(2,128)(2,1)}), bf16[32,2,16384]{2,1,0:T(2,128)(2,1)}, u32[]{:S(2)}, u32[]{:S(2)}) %all-to-all-start.1) | async-done | bytes 2097184 | tf_op jit(solution)/shard_map/all_to_all | solution.py:57
  204.2 6.5 %all-to-all-start.2 = ((bf16[32,2,16384]{2,1,0:T(2,128)(2,1)}), bf16[32,2,16384]{2,1,0:T(2,128)(2,1)}, u32[]{:S(2)}, u32[]{:S(2)}) async-start(bf16[32,2,16384]{2,1,0:T(2,128)(2,1)} %reshape.72), calls=%async_computation.2 | async-start | bytes 4194304 | tf_op jit(solution)/shard_map/all_to_all | solution.py:59
  210.7 0.0 copy-done.2
  210.7 0.0 copy-done.3
  210.7 40.2 %all-gather.1 = bf16[16,64,16]{1,2,0:T(8,128)(2,1)S(1)} all-gather(bf16[1,64,16]{1,2,0:T(8,128)(2,1)S(1)} %fusion), channel_id=2, replica_groups=mesh['bank'=4,'zero_0'=4,'zero_1'=4,'zero_2'=2] {'zero_0','zero_1'}, dimensions={0}, use_global_device_ids=true | all-gather | bytes 34816 | tf_op jit(solution)/shard_map/all_gather | solution.py:27
  250.9 6.5 %all_gather.10 = bf16[32,64,16]{1,2,0:T(8,128)(2,1)S(1)} all-gather(bf16[16,64,16]{1,2,0:T(8,128)(2,1)S(1)} %all-gather.1), channel_id=1, replica_groups=mesh['bank'=4,'zero_0'=4,'zero_1'=4,'zero_2'=2] {'zero_2'}, dimensions={0}, use_global_device_ids=true | all-gather | bytes 98304 | tf_op jit(solution)/shard_map/all_gather | solution.py:27
  257.5 0.1 copy.39
  257.6 0.2 reshape_reshape.3
  257.8 10.3 %all_gather.11 = bf16[2048,64]{0,1:T(8,128)(2,1)S(1)} all-gather(bf16[2048,16]{0,1:T(8,128)(2,1)S(1)} %reshape_reshape.3), channel_id=1, replica_groups=mesh['bank'=4,'zero_0'=4,'zero_1'=4,'zero_2'=2] {'bank'}, dimensions={1}, use_global_device_ids=true | all-gather | bytes 327680 | tf_op jit(solution)/shard_map/all_gather | solution.py:71
  268.1 0.7 constant_dynamic-slice_fusion.2
  268.7 0.7 constant_dynamic-slice_fusion
  269.4 4.0 %reshape.69 = bf16[1024,16,64]{2,1,0:T(8,128)(2,1)} reshape(bf16[32,2,16384]{2,1,0:T(2,128)(2,1)S(1)} %all-to-all-done) | data formatting | bytes 4194304
  273.4 6.9 %copy.30 = bf16[16,32,64,32]{2,1,3,0:T(8,128)(2,1)} copy(bf16[16,32,64,32]{2,0,3,1:T(8,128)(2,1)} %bitcast.41) | data formatting | bytes 4194304 | tf_op jit(solution)/shard_map/all_to_all | solution.py:56
  280.2 6.7 %all_to_all.42 = bf16[16,2048,32]{1,2,0:T(8,128)(2,1)} reshape(bf16[16,32,64,32]{2,1,3,0:T(8,128)(2,1)} %copy.30) | data formatting | bytes 4194304 | tf_op jit(solution)/shard_map/all_to_all | solution.py:56
  287.0 7.9 %reshape.71 = bf16[1024,16,64]{2,1,0:T(8,128)(2,1)} reshape(bf16[32,2,16384]{2,1,0:T(2,128)(2,1)} %all-to-all-done.1) | data formatting | bytes 4194304
  294.9 6.9 %copy.34 = bf16[16,32,64,32]{2,1,3,0:T(8,128)(2,1)} copy(bf16[16,32,64,32]{2,0,3,1:T(8,128)(2,1)} %bitcast.42) | data formatting | bytes 4194304 | tf_op jit(solution)/shard_map/all_to_all | solution.py:57
  301.8 6.7 %all_to_all.46 = bf16[16,2048,32]{1,2,0:T(8,128)(2,1)} reshape(bf16[16,32,64,32]{2,1,3,0:T(8,128)(2,1)} %copy.34) | data formatting | bytes 4194304 | tf_op jit(solution)/shard_map/all_to_all | solution.py:57
  308.5 0.0 all-to-all-done.2
  308.5 7.9 %reshape.73 = bf16[1024,16,64]{2,1,0:T(8,128)(2,1)} reshape(bf16[32,2,16384]{2,1,0:T(2,128)(2,1)} %all-to-all-done.2) | data formatting | bytes 4194304
  316.5 6.9 %copy.38 = bf16[16,32,32,64]{3,2,1,0:T(8,128)(2,1)} copy(bf16[16,32,32,64]{3,0,1,2:T(8,128)(2,1)} %bitcast.43) | data formatting | bytes 4194304 | tf_op jit(solution)/shard_map/all_to_all | solution.py:59
  323.3 6.7 %all_to_all.50 = bf16[16,32,2048]{2,1,0:T(8,128)(2,1)} reshape(bf16[16,32,32,64]{3,2,1,0:T(8,128)(2,1)} %copy.38) | data formatting | bytes 4194304 | tf_op jit(solution)/shard_map/all_to_all | solution.py:59
  330.1 0.7 copy.48
  (7 shorter events, 0.1 us)
Async XLA Ops:
  7.2 112.3 %all-reduce.2.cloned.1.call-start = ((), (), s32[]{:S(2)}) async-start(), calls=%async_computation.3 | async-start | bytes 393216 | tf_op jit(solution)/shard_map/psum | solution.py:14
  7.2 3.5 %copy-start = (f32[16,64,1024]{2,1,0:T(8,128)S(1)}, f32[16,64,1024]{2,1,0:T(8,128)}, u32[]{:S(2)}) copy-start(f32[16,64,1024]{2,1,0:T(8,128)} %param.6) | copy-start | bytes 12582916
  7.2 4.7 %copy-start.1 = (f32[16,1024,64]{1,2,0:T(8,128)S(1)}, f32[16,1024,64]{1,2,0:T(8,128)}, u32[]{:S(2)}) copy-start(f32[16,1024,64]{1,2,0:T(8,128)} %param.7) | copy-start | bytes 12582916
  135.4 34.7 %all-to-all-start = ((bf16[32,2,16384]{2,1,0:T(2,128)(2,1)}), bf16[32,2,16384]{2,1,0:T(2,128)(2,1)S(1)}, u32[]{:S(2)}, u32[]{:S(2)}) async-start(bf16[32,2,16384]{2,1,0:T(2,128)(2,1)} %reshape.68), calls=%async_computation | async-start | bytes 4194304 | tf_op jit(solution)/shard_map/all_to_all | solution.py:56
  170.1 34.1 %all-to-all-start.1 = ((bf16[32,2,16384]{2,1,0:T(2,128)(2,1)}), bf16[32,2,16384]{2,1,0:T(2,128)(2,1)}, u32[]{:S(2)}, u32[]{:S(2)}) async-start(bf16[32,2,16384]{2,1,0:T(2,128)(2,1)} %reshape.70), calls=%async_computation.1 | async-start | bytes 4194304 | tf_op jit(solution)/shard_map/all_to_all | solution.py:57
  190.5 20.1 %copy-start.2 = (f32[64,16]{0,1:T(8,128)S(1)}, f32[64,16]{0,1:T(8,128)}, u32[]{:S(2)}) copy-start(f32[64,16]{0,1:T(8,128)} %param.8) | copy-start | bytes 12292
  190.5 20.1 %copy-start.3 = (f32[64]{0:T(128)S(1)}, f32[64]{0:T(128)}, u32[]{:S(2)}) copy-start(f32[64]{0:T(128)} %param.9) | copy-start | bytes 772
  204.2 104.4 %all-to-all-start.2 = ((bf16[32,2,16384]{2,1,0:T(2,128)(2,1)}), bf16[32,2,16384]{2,1,0:T(2,128)(2,1)}, u32[]{:S(2)}, u32[]{:S(2)}) async-start(bf16[32,2,16384]{2,1,0:T(2,128)(2,1)} %reshape.72), calls=%async_computation.2 | async-start | bytes 4194304 | tf_op jit(solution)/shard_map/all_to_all | solution.py:59
Sparse Core Ops, SparseCore 0:
  13.4 106.0 all-reduce.1
where the time goes:
time: 341 us; the launch traced here: 338 us
  local copies, waits for them, and re-layouts  114 us (33%)
  waiting for transfers between devices  110 us (32%)
  blocking collectives  57 us (17%)
  other arithmetic  25.5 us (7%)
  starting transfers between devices  17.3 us (5%)
  between operations  14.2 us (4%)
    psum x1, waiting for transfers between devices, packed_total(): total = lax.psum(jnp.concatenate([a.ravel() for a in arrays]), axis)  98.1 us
    unnamed x21, local copies, waits for them, and re-layouts  69.7 us
    all_gather x2, blocking collectives, all_blocks(): pieces = lax.all_gather(pieces, axes[k], axis=0, tiled=True)  46.8 us
    unnamed x4, other arithmetic  20.6 us
    all_to_all x2, local copies, waits for them, and re-layouts, body(): lax.all_to_all(narrow_down, ZERO, split_axis=1, concat_axis=2, tiled=True)  13.6 us
    all_to_all x2, local copies, waits for them, and re-layouts, body(): lax.all_to_all(narrow_gate, ZERO, split_axis=2, concat_axis=1, tiled=True)  13.6 us
    all_to_all x2, local copies, waits for them, and re-layouts, body(): lax.all_to_all(narrow_up, ZERO, split_axis=2, concat_axis=1, tiled=True)  13.6 us
    all_gather x1, blocking collectives, body(): serve_router = lax.all_gather(row_router, 'bank', axis=1, tiled=True)  10.3 us
  transfers between devices with their start and end apart: 4, of which 3 were waited for; matrix products, arithmetic and copies ran while one was open for 24% of the time, Pallas kernels for 0%

commit v1 on v0

v1 whole, which is shorter than its diff:
```python
import jax
import jax.numpy as jnp
from jax import lax
from jax.experimental import pallas as pl
from jax.experimental.pallas import tpu as pltpu
from jax.sharding import PartitionSpec as P

MESH = pl.DeviceIdType.MESH
ZERO = 32
CHUNKS = 6
PAIRS = 24
PER = PAIRS // CHUNKS
ROWS = PER * 32
POWER = 20
UP = 2.0**6.25
ORDER = (
    (0, 1), (3, 0), (2, 3), (1, 1), (3, 3), (0, 2), (1, 0), (3, 1),
    (1, 3), (2, 2), (2, 0), (0, 3), (1, 2), (3, 2), (2, 1),
)
OFFSETS = tuple((z, x, c) for z, x in ORDER for c in (0, 1))


def exchange(
    gate, up, down, weight, gain,
    out, scale, router,
    xin, send, recv, sums, sums_send, sums_recv, table, part_send, part_recv,
    in_sem, send_sem, recv_sem, sums_send_sem, sums_recv_sem,
    part_send_sem, part_recv_sem, row_send_sem, row_recv_sem,
):
    me = lax.axis_index("zero")
    bank = lax.axis_index("bank")
    mz, mx, mc = lax.div(me, 8), lax.rem(lax.div(me, 2), 4), lax.rem(me, 2)

    def peer(offset):
        z, x, c = offset
        return (
            lax.rem(mz + z, 4) * 8 + lax.rem(mx + x, 4) * 2 + lax.rem(mc + c, 2)
        )

    loads = []
    for a, ref in enumerate((gate, up, down)):
        for h in range(2):
            copy = pltpu.make_async_copy(
                ref.at[pl.ds(8 * h, 8)],
                xin.at[pl.ds(16 * a + 8 * h, 8)],
                in_sem.at[2 * a + h],
            )
            copy.start()
            loads.append(copy)

    barrier = pltpu.get_barrier_semaphore()

    def greet(i, _):
        pl.semaphore_signal(
            barrier,
            inc=1,
            device_id={"zero": lax.rem(me + i, ZERO)},
            device_id_type=MESH,
        )
        return 0

    lax.fori_loop(1, ZERO, greet, 0)
    for i in range(1, 4):
        pl.semaphore_signal(
            barrier,
            inc=1,
            device_id={"bank": lax.rem(bank + i, 4)},
            device_id_type=MESH,
        )

    part = (weight[...] * gain[...]).astype(jnp.bfloat16)
    packed = jnp.concatenate([part[0:8], part[8:16]], axis=1)
    part_send[...] = packed
    part_recv[me] = packed

    def add_up(e, _):
        x = xin[e]
        sums[e] = jnp.sum(x * x, axis=0, keepdims=True)
        return 0

    def code_pair(c):
        def go(k, _):
            p = c * PER + k
            for b in range(8):
                columns = slice(128 * b, 128 * b + 128)
                halves = []
                for e in range(2):
                    s = sums[2 * p + e, :, columns]
                    r = jnp.where(s > 0.0, lax.rsqrt(s) * UP, 0.0)
                    halves.append(xin[2 * p + e, :, columns] * r)
                y = jnp.concatenate(halves, axis=0).T
                y2 = y * y
                y4 = y2 * y2
                y8 = y4 * y4
                y20 = y8 * y8 * y4
                u = jnp.where(y < 0.0, -y20, y20).astype(jnp.bfloat16)
                for q in range(4):
                    send[c, 4 * b + q, pl.ds(pl.multiple_of(32 * k, 32), 32), :] = u[
                        32 * q : 32 * q + 32
                    ]
            return 0

        return go

    def send_chunk(c):
        for offset in OFFSETS:
            d = peer(offset)
            pltpu.make_async_remote_copy(
                src_ref=send.at[c, d],
                dst_ref=recv.at[c, me],
                send_sem=send_sem.at[c],
                recv_sem=recv_sem.at[c],
                device_id={"zero": d},
                device_id_type=MESH,
            ).start()
        d = peer((0, 0, 1))
        pltpu.make_async_remote_copy(
            src_ref=send.at[c, d],
            dst_ref=recv.at[c, me],
            send_sem=send_sem.at[c],
            recv_sem=recv_sem.at[c],
            device_id={"zero": d},
            device_id_type=MESH,
        ).start()
        recv[c, me] = send[c, me]

    loads[0].wait()
    lax.fori_loop(0, 8, add_up, 0)
    lax.fori_loop(0, PER, code_pair(0), 0)
    pl.semaphore_wait(barrier, ZERO - 1 + 3)
    send_chunk(0)

    for i in range(1, 6):
        loads[i].wait()
        lax.fori_loop(8 * i, 8 * i + 8, add_up, 0)

    pad = jnp.zeros((16, 128), jnp.float32)
    for b in range(8):
        s = sums[:, 0, 128 * b : 128 * b + 128]
        t = jnp.concatenate([s, pad, pltpu.roll(s, 112, 1), pad], axis=0).T
        for q in range(4):
            sums_send[4 * b + q] = t[32 * q : 32 * q + 16]
    for offset in OFFSETS + ((0, 0, 1),):
        d = peer(offset)
        pltpu.make_async_remote_copy(
            src_ref=sums_send.at[d],
            dst_ref=sums_recv.at[me],
            send_sem=sums_send_sem,
            recv_sem=sums_recv_sem,
            device_id={"zero": d},
            device_id_type=MESH,
        ).start()
        pltpu.make_async_remote_copy(
            src_ref=part_send,
            dst_ref=part_recv.at[me],
            send_sem=part_send_sem,
            recv_sem=part_recv_sem,
            device_id={"zero": d},
            device_id_type=MESH,
        ).start()
    sums_recv[me] = sums_send[me]

    def code_and_send(c, _):
        lax.fori_loop(0, PER, code_pair(c), 0)
        send_chunk(c)
        return 0

    lax.fori_loop(1, CHUNKS, code_and_send, 0)

    others = pl.ds(0, ZERO - 1)
    pltpu.make_async_copy(
        sums_recv.at[others], sums_recv.at[others], sums_recv_sem
    ).wait()
    total = sums_recv[0]
    for s in range(1, ZERO):
        total = total + sums_recv[s]
    root = jnp.sqrt(jnp.concatenate([total] + [jnp.zeros((112, 128), jnp.float32)], 0).T)
    first, second = root[0:48], pltpu.roll(root[64:112], 16, 1)
    lane = lax.broadcasted_iota(jnp.int32, (48, 128), 1)
    scale[...] = jnp.where(lane < 16, first, second)[:, 0:32]

    for n in range(16):
        rows = jnp.concatenate(
            [sums_recv[:, n, :], jnp.zeros((96, 128), jnp.float32)], axis=0
        ).T
        whole = jnp.sum(rows, axis=1, keepdims=True)
        ratio = jnp.sqrt(rows) * lax.rsqrt(whole) * (1.0 / UP)
        table[:, n, :] = ratio[0:64]
        table[:, n + 16, :] = ratio[64:128]

    half = lax.broadcasted_iota(jnp.int32, (32, 128), 1) < 64

    def decode_pair(c):
        def go(k, _):
            p = c * PER + k
            rows = pl.ds(pl.multiple_of(32 * k, 32), 32)
            f0 = table[2 * p]
            f1 = table[2 * p + 1]
            for t in range(16):
                columns = slice(128 * t, 128 * t + 128)
                a = recv[c, 2 * t, rows, :].astype(jnp.float32)
                b = recv[c, 2 * t + 1, rows, :].astype(jnp.float32)
                for e, f, u in (
                    (0, f0, jnp.where(half, a, pltpu.roll(b, 64, 1))),
                    (1, f1, jnp.where(half, pltpu.roll(a, 64, 1), b)),
                ):
                    g = jnp.where(
                        half,
                        jnp.broadcast_to(f[:, 2 * t : 2 * t + 1], (32, 128)),
                        jnp.broadcast_to(f[:, 2 * t + 1 : 2 * t + 2], (32, 128)),
                    )
                    m = jnp.exp(jnp.log(jnp.abs(u)) * (1.0 / POWER))
                    v = jnp.where(u < 0.0, -m, m) * g
                    out[2 * p + e, :, columns] = v.astype(jnp.bfloat16)
            return 0

        return go

    pltpu.make_async_copy(
        part_recv.at[others], part_recv.at[others], part_recv_sem
    ).wait()
    mine = pl.ds(pl.multiple_of(16 * bank, 16), 16)
    for t in range(16):
        a = part_recv[2 * t].astype(jnp.float32)
        b = part_recv[2 * t + 1].astype(jnp.float32)
        low = half[0:8]
        block = jnp.concatenate(
            [
                jnp.where(low, a, pltpu.roll(b, 64, 1)),
                jnp.where(low, pltpu.roll(a, 64, 1), b),
            ],
            axis=0,
        )
        router[mine, 128 * t : 128 * t + 128] = block.astype(jnp.bfloat16)
    rows_out = []
    for i in range(1, 4):
        copy = pltpu.make_async_remote_copy(
            src_ref=router.at[mine],
            dst_ref=router.at[mine],
            send_sem=row_send_sem,
            recv_sem=row_recv_sem,
            device_id={"bank": lax.rem(bank + i, 4)},
            device_id_type=MESH,
        )
        copy.start()
        rows_out.append(copy)

    def receive(c, _):
        pltpu.make_async_copy(
            recv.at[c, others], recv.at[c, others], recv_sem.at[c]
        ).wait()
        lax.fori_loop(0, PER, decode_pair(c), 0)
        return 0

    lax.fori_loop(0, CHUNKS, receive, 0)

    three = pl.ds(0, 48)
    pltpu.make_async_copy(router.at[three], router.at[three], row_recv_sem).wait()
    pltpu.make_async_copy(router.at[three], router.at[three], row_send_sem).wait()
    pltpu.make_async_copy(
        sums_send.at[others], sums_send.at[others], sums_send_sem
    ).wait()
    pltpu.make_async_copy(
        part_recv.at[others], part_recv.at[others], part_send_sem
    ).wait()

    def drain(c, _):
        pltpu.make_async_copy(
            send.at[c, others], send.at[c, others], send_sem.at[c]
        ).wait()
        return 0

    lax.fori_loop(0, CHUNKS, drain, 0)


def hand_out(out, scale, router, gate, up, down, sg, su, sd, served, sem):
    copies = [pltpu.make_async_copy(router, served, sem.at[0])]
    for a, (big, small) in enumerate(((gate, sg), (up, su), (down, sd))):
        part = pl.ds(16 * a, 16)
        copies.append(pltpu.make_async_copy(out.at[part], big, sem.at[2 * a + 1]))
        copies.append(pltpu.make_async_copy(scale.at[part], small, sem.at[2 * a + 2]))
    for copy in copies:
        copy.start()
    for copy in copies:
        copy.wait()


def body(gate, up, down, weight, gain):
    vmem = pl.BlockSpec(memory_space=pltpu.VMEM)
    hbm = pl.BlockSpec(memory_space=pltpu.HBM)
    f32, bf16 = jnp.float32, jnp.bfloat16
    dma, plain = pltpu.SemaphoreType.DMA, pltpu.SemaphoreType.REGULAR
    out, scale, router = pl.pallas_call(
        exchange,
        name="exchange",
        out_shape=(
            pltpu.VMEM((48, 32, 2048), bf16),
            pltpu.VMEM((48, 32), f32),
            pltpu.VMEM((64, 2048), bf16),
        ),
        in_specs=[hbm, hbm, hbm, vmem, vmem],
        out_specs=(vmem, vmem, vmem),
        scratch_shapes=[
            pltpu.VMEM((48, 64, 1024), f32),
            pltpu.VMEM((CHUNKS, ZERO, ROWS, 128), bf16),
            pltpu.VMEM((CHUNKS, ZERO, ROWS, 128), bf16),
            pltpu.VMEM((48, 1, 1024), f32),
            pltpu.VMEM((ZERO, 16, 128), f32),
            pltpu.VMEM((ZERO, 16, 128), f32),
            pltpu.VMEM((64, 32, 128), f32),
            pltpu.VMEM((8, 128), bf16),
            pltpu.VMEM((ZERO, 8, 128), bf16),
            dma((6,)),
            dma((CHUNKS,)),
            dma((CHUNKS,)),
            dma,
            dma,
            dma,
            dma,
            dma,
            dma,
        ],
        compiler_params=pltpu.CompilerParams(
            collective_id=0, has_side_effects=True, vmem_limit_bytes=48 * 2**20
        ),
    )(gate, up, jnp.swapaxes(down, 1, 2), weight.T, gain.reshape(1, 64))
    half = jax.ShapeDtypeStruct((16, 32, 2048), bf16)
    few = jax.ShapeDtypeStruct((16, 32), f32)
    gate, up, down, sg, su, sd, served = pl.pallas_call(
        hand_out,
        name="hand_out",
        out_shape=(half, half, half, few, few, few, jax.ShapeDtypeStruct((64, 2048), bf16)),
        in_specs=[pl.BlockSpec(memory_space=pl.ANY)] * 3,
        out_specs=(hbm,) * 7,
        scratch_shapes=[dma((7,))],
    )(out, scale, router)
    return (
        jnp.swapaxes(gate, 1, 2),
        jnp.swapaxes(up, 1, 2),
        down,
        sg,
        su,
        sd,
        served.T,
    )


def solution(mesh):
    return jax.shard_map(
        body,
        mesh=mesh,
        in_specs=(
            P("bank", "zero", None),
            P("bank", "zero", None),
            P("bank", None, "zero"),
            P("zero", "bank"),
            P("zero"),
        ),
        out_specs=(
            P("bank", None, "zero"),
            P("bank", None, "zero"),
            P("bank", "zero", None),
            P("bank", "zero"),
            P("bank", "zero"),
            P("bank", "zero"),
            P(),
        ),
        check_vma=False,
    )
```

time: 341 us -> 294 us (0.86)
  Pallas kernels: 0 us -> 287 us
  local copies, waits for them, and re-layouts: 114 us -> 3.95 us
  waiting for transfers between devices: 110 us -> 0 us
  blocking collectives: 57 us -> 0 us
  other arithmetic: 25.5 us -> 0 us
  starting transfers between devices: 17.3 us -> 0 us
  between operations: 14.2 us -> 0.65 us
    pallas_call x0 -> x2, Pallas kernels: none -> 287 us  [the longest x1 200 us: body(): pl.pallas_call(hand_out, name='hand_out', out_shape=(half, half, half, fe...]
    psum x1 -> x0, waiting for transfers between devices: 98.1 us -> none  [packed_total(): total = lax.psum(jnp.concatenate([a.ravel() for a in arrays]), axis)]
    unnamed x21 -> x6, local copies, waits for them, and re-layouts: 69.7 us -> 3.95 us
    all_gather x3 -> x0, blocking collectives: 57 us -> none  [the longest x2 46.8 us: all_blocks(): pieces = lax.all_gather(pieces, axes[k], axis=0, tiled=True)]
    all_to_all x6 -> x0, local copies, waits for them, and re-layouts: 40.8 us -> none  [the longest x2 13.6 us: body(): lax.all_to_all(narrow_down, ZERO, split_axis=1, concat_axis=2, tiled=True)]
    unnamed x4 -> x0, other arithmetic: 20.6 us -> none
    all_to_all x3 -> x0, starting transfers between devices: 17.2 us -> none  [the longest x1 6.46 us: body(): lax.all_to_all(narrow_down, ZERO, split_axis=1, concat_axis=2, tiled=True)]
    all_to_all x3 -> x0, waiting for transfers between devices: 11.8 us -> none  [the longest x1 6.05 us: body(): lax.all_to_all(narrow_gate, ZERO, split_axis=2, concat_axis=1, tiled=True)]
  transfers between devices with their start and end apart: 4 -> 0, of which waited for: 3 -> 0; matrix products, arithmetic and copies ran while one was open for 24% -> 0% of each run, Pallas kernels for 0% -> 0%
where the time goes in v1:
time: 294 us; the launch traced here: 292 us
  Pallas kernels  287 us (98%)
  local copies, waits for them, and re-layouts  3.95 us (1%)
    pallas_call x1, Pallas kernels, body(): pl.pallas_call(hand_out, name='hand_out', out_shape=(half, half, half, fe...  200 us
    pallas_call x1, Pallas kernels, body(): pl.pallas_call(exchange, name='exchange', out_shape=(pltpu.VMEM((48, 32,...  86.7 us

profile of v1, /device:TPU:1, one launch (start us, length us, event | category | flops | bytes accessed | tf_op | source)
XLA Modules:
  0.0 291.7 jit_solution(1279230639590608808)
XLA Ops:
  0.6 86.7 %exchange.1 = (bf16[48,32,2048]{2,1,0:T(8,128)(2,1)S(1)}, f32[48,32]{1,0:T(8,128)S(1)}, bf16[64,2048]{1,0:T(8,128)(2,1)S(1)}) custom-call(f32[16,64,1024]{2,1,0:T(8,128)} %gate.1, f32[16,64,1024]{2,1,0:T(8,128)} %up.1, f32[16,64,1024]{2,1,0:T(8,128)} %bitcast.6, f32[16,64]{1,0:T(8,128)} %bitcast.7, f32[1,64]{1,0:T(1,128)} %bitcast.8), custom_call_target="tpu_custom_call" | custom-call | tf_op jit(solution)/shard_map/exchange/pallas_call | solution.py:293
  87.3 0.0 copy-start
  87.3 2.6 copy-done
  90.0 0.0 copy-start.1
  90.0 0.7 copy-done.1
  90.7 0.0 copy-start.2
  90.7 0.6 copy-done.2
  91.3 200.4 %hand_out.1 = (bf16[16,32,2048]{2,1,0:T(8,128)(2,1)}, bf16[16,32,2048]{2,1,0:T(8,128)(2,1)}, bf16[16,32,2048]{2,1,0:T(8,128)(2,1)}, f32[16,32]{1,0:T(8,128)}, f3...) custom-call(bf16[48,32,2048]{2,1,0:T(8,128)(2,1)} %copy-done, f32[48,32]{1,0:T(8,128)} %copy-done.2, ...), custom_call_target="tpu_custom_call" | custom-call | tf_op jit(solution)/shard_map/hand_out/pallas_call | solution.py:329
Async XLA Ops:
  87.3 2.7 copy-start
  90.0 0.7 copy-start.1
  90.7 0.6 copy-start.2

commit v2 on v1

--- a/solution.py
+++ b/solution.py
@@ -330,10 +330,11 @@
         hand_out,
         name="hand_out",
         out_shape=(half, half, half, few, few, few, jax.ShapeDtypeStruct((64, 2048), bf16)),
-        in_specs=[pl.BlockSpec(memory_space=pl.ANY)] * 3,
+        in_specs=[vmem] * 3,
         out_specs=(hbm,) * 7,
         scratch_shapes=[dma((7,))],
-    )(out, scale, router)
+        compiler_params=pltpu.CompilerParams(vmem_limit_bytes=16 * 2**20),
+    )(*(pltpu.with_memory_space_constraint(a, pltpu.VMEM) for a in (out, scale, router)))
     return (
         jnp.swapaxes(gate, 1, 2),
         jnp.swapaxes(up, 1, 2),

time: 294 us -> 92.4 us (0.31)
  the two profiles are of different devices: /device:TPU:1 before, /device:TPU:3 now
where the time goes in v2:
time: 92.4 us; the launch traced here: 92.3 us
  Pallas kernels  91.6 us (99%)
    pallas_call x1, Pallas kernels, body(): pl.pallas_call(exchange, name='exchange', out_shape=(pltpu.VMEM((48, 32,...  88.8 us
    pallas_call x1, Pallas kernels, body(): pl.pallas_call(hand_out, name='hand_out', out_shape=(half, half, half, fe...  2.86 us

profile of v2, /device:TPU:3, one launch (start us, length us, event | category | flops | bytes accessed | tf_op | source)
XLA Modules:
  0.0 92.3 jit_solution(12464802042857515180)
XLA Ops:
  0.6 88.8 %exchange.1 = (bf16[48,32,2048]{2,1,0:T(8,128)(2,1)S(1)}, f32[48,32]{1,0:T(8,128)S(1)}, bf16[64,2048]{1,0:T(8,128)(2,1)S(1)}) custom-call(f32[16,64,1024]{2,1,0:T(8,128)} %gate.1, f32[16,64,1024]{2,1,0:T(8,128)} %up.1, f32[16,64,1024]{2,1,0:T(8,128)} %bitcast.6, f32[16,64]{1,0:T(8,128)} %bitcast.7, f32[1,64]{1,0:T(1,128)} %bitcast.8), custom_call_target="tpu_custom_call" | custom-call | tf_op jit(solution)/shard_map/exchange/pallas_call | solution.py:293
  89.4 2.9 %hand_out.1 = (bf16[16,32,2048]{2,1,0:T(8,128)(2,1)}, bf16[16,32,2048]{2,1,0:T(8,128)(2,1)}, bf16[16,32,2048]{2,1,0:T(8,128)(2,1)}, f32[16,32]{1,0:T(8,128)}, f3...) custom-call(bf16[48,32,2048]{2,1,0:T(8,128)(2,1)S(1)} %get-tuple-element.17.out, ...), custom_call_target="tpu_custom_call" | custom-call | tf_op jit(solution)/shard_map/hand_out/pallas_call | solution.py:329

commit v3 on v2

v3 whole, which is shorter than its diff:
```python
import jax
import jax.numpy as jnp
from jax import lax
from jax.experimental import pallas as pl
from jax.experimental.pallas import tpu as pltpu
from jax.sharding import PartitionSpec as P

MESH = pl.DeviceIdType.MESH
CHUNKS = 6
PAIRS = 24
PER = PAIRS // CHUNKS // 2
ROWS = PER * 32
POWER = 20
UP = 2.0**6.25


def exchange(
    gate, up, down, weight, gain,
    out, scale, router,
    xin, send, relay, recv, sums, sums_send, sums_relay, sums_recv, table, parts,
    in_sem, send_sem, relay_sem, pass_sem, recv_sem,
    sums_send_sem, sums_relay_sem, sums_pass_sem, sums_recv_sem,
    parts_send_sem, parts_recv_sem, row_send_sem, row_recv_sem,
):
    me = lax.axis_index("zero")
    bank = lax.axis_index("bank")
    mz, mx, mc = lax.div(me, 8), lax.rem(lax.div(me, 2), 4), lax.rem(me, 2)
    mate = 1 - mc

    def turn(place, i):
        return lax.rem(place + i, 4)

    def device(z, x, c):
        return z * 8 + x * 2 + c

    def put(src, dst, sent, arrived, z, x, c):
        pltpu.make_async_remote_copy(
            src_ref=src,
            dst_ref=dst,
            send_sem=sent,
            recv_sem=arrived,
            device_id={"zero": device(z, x, c)},
            device_id_type=MESH,
        ).start()

    def wait(ref, sem):
        pltpu.make_async_copy(ref, ref, sem).wait()

    loads = []
    for a, ref in enumerate((gate, up, down)):
        for h in range(2):
            copy = pltpu.make_async_copy(
                ref.at[pl.ds(8 * h, 8)],
                xin.at[pl.ds(16 * a + 8 * h, 8)],
                in_sem.at[2 * a + h],
            )
            copy.start()
            loads.append(copy)

    barrier = pltpu.get_barrier_semaphore()

    def greet(**where):
        pl.semaphore_signal(
            barrier, inc=1, device_id=where, device_id_type=MESH
        )

    greet(zero=device(mz, mx, mate))
    for i in (1, 3, 2):
        for c in range(2):
            greet(zero=device(turn(mz, i), mx, c))
            greet(zero=device(mz, turn(mx, i), c))
        greet(bank=turn(bank, i))

    part = (weight[...] * gain[...]).astype(jnp.bfloat16)
    parts[mc, mz, mx] = jnp.concatenate([part[0:8], part[8:16]], axis=1)

    def add_up(e, _):
        x = xin[e]
        sums[e] = jnp.sum(x * x, axis=0, keepdims=True)
        return 0

    def code_pair(c, h):
        def go(k, _):
            p = (2 * c + h) * PER + k
            rows = pl.ds(pl.multiple_of(32 * k, 32), 32)
            for b in range(8):
                columns = slice(128 * b, 128 * b + 128)
                halves = []
                for e in range(2):
                    s = sums[2 * p + e, :, columns]
                    r = jnp.where(s > 0.0, lax.rsqrt(s) * UP, 0.0)
                    halves.append(xin[2 * p + e, :, columns] * r)
                y = jnp.concatenate(halves, axis=0).T
                y2 = y * y
                y4 = y2 * y2
                y8 = y4 * y4
                y20 = y8 * y8 * y4
                u = jnp.where(y < 0.0, -y20, y20).astype(jnp.bfloat16)
                for q in range(4):
                    z, x, d = b // 2, b % 2 * 2 + q // 2, q % 2
                    first, second = ((x, z), (z, x))[h]
                    send[h, c, first, 2 * second + d, rows, :] = u[32 * q : 32 * q + 32]
            return 0

        return go

    def code(c):
        for h in range(2):
            lax.fori_loop(0, PER, code_pair(c, h), 0)

    def leave(c):
        for i in (1, 3, 2):
            x, z = turn(mx, i), turn(mz, i)
            put(send.at[0, c, x], relay.at[0, c, mx], send_sem, relay_sem.at[0, c], mz, x, mc)
            put(send.at[1, c, z], relay.at[1, c, mz], send_sem, relay_sem.at[1, c], z, mx, mc)
        relay[0, c, mx] = send[0, c, mx]
        relay[1, c, mz] = send[1, c, mz]

    four = pl.ds(0, 4)
    three = pl.ds(0, 3)

    def go_on(c):
        for h in range(2):
            wait(relay.at[h, c, three], relay_sem.at[h, c])
        at_z, at_x = 2 * mz + mc, 2 * mx + mc
        for i in (1, 3, 2):
            for d in range(2):
                x, z = turn(mx, i), turn(mz, i)
                put(relay.at[0, c, four, 2 * z + d], recv.at[0, c, at_z], pass_sem, recv_sem.at[0, c], z, mx, d)
                put(relay.at[1, c, four, 2 * x + d], recv.at[1, c, at_x], pass_sem, recv_sem.at[1, c], mz, x, d)
        put(relay.at[0, c, four, 2 * mz + mate], recv.at[0, c, at_z], pass_sem, recv_sem.at[0, c], mz, mx, mate)
        put(relay.at[1, c, four, 2 * mx + mate], recv.at[1, c, at_x], pass_sem, recv_sem.at[1, c], mz, mx, mate)
        recv[0, c, at_z] = relay[0, c, :, at_z]
        recv[1, c, at_x] = relay[1, c, :, at_x]

    loads[0].wait()
    lax.fori_loop(0, 8, add_up, 0)
    code(0)
    pl.semaphore_wait(barrier, 16)
    leave(0)

    for i in range(1, 6):
        loads[i].wait()
        lax.fori_loop(8 * i, 8 * i + 8, add_up, 0)

    pad = jnp.zeros((16, 128), jnp.float32)
    for b in range(8):
        s = sums[:, 0, 128 * b : 128 * b + 128]
        t = jnp.concatenate([s, pad, pltpu.roll(s, 112, 1), pad], axis=0).T
        for q in range(4):
            z, x, d = b // 2, b % 2 * 2 + q // 2, q % 2
            sums_send[x, 2 * z + d] = t[32 * q : 32 * q + 16]
    for i in (1, 3, 2):
        x = turn(mx, i)
        put(sums_send.at[x], sums_relay.at[mx], sums_send_sem, sums_relay_sem, mz, x, mc)
        put(parts.at[mc, mz, mx], parts.at[mc, mz, mx], parts_send_sem.at[0], parts_recv_sem.at[0], mz, x, mc)
    sums_relay[mx] = sums_send[mx]

    code(1)
    leave(1)

    wait(sums_relay.at[three], sums_relay_sem)
    wait(parts.at[0, 0, three], parts_recv_sem.at[0])
    at_z = 2 * mz + mc
    for i in (1, 3, 2):
        z = turn(mz, i)
        for d in range(2):
            put(sums_relay.at[four, 2 * z + d], sums_recv.at[at_z], sums_pass_sem, sums_recv_sem, z, mx, d)
        put(parts.at[mc, mz], parts.at[mc, mz], parts_send_sem.at[1], parts_recv_sem.at[1], z, mx, mc)
    put(sums_relay.at[four, 2 * mz + mate], sums_recv.at[at_z], sums_pass_sem, sums_recv_sem, mz, mx, mate)
    sums_recv[at_z] = sums_relay[:, at_z]

    go_on(0)
    code(2)
    leave(2)

    wait(sums_recv.at[pl.ds(0, 7)], sums_recv_sem)
    total = jnp.zeros((16, 128), jnp.float32)
    for s in range(32):
        total = total + sums_recv[s // 4, s % 4]
    root = jnp.sqrt(jnp.concatenate([total] + [jnp.zeros((112, 128), jnp.float32)], 0).T)
    first, second = root[0:48], pltpu.roll(root[64:112], 16, 1)
    lane = lax.broadcasted_iota(jnp.int32, (48, 128), 1)
    scale[...] = jnp.where(lane < 16, first, second)[:, 0:32]

    for n in range(16):
        rows = jnp.concatenate(
            [
                sums_recv[:, :, n, :].reshape(32, 128),
                jnp.zeros((96, 128), jnp.float32),
            ],
            axis=0,
        ).T
        whole = jnp.sum(rows, axis=1, keepdims=True)
        ratio = jnp.sqrt(rows) * lax.rsqrt(whole) * (1.0 / UP)
        table[:, n, :] = ratio[0:64]
        table[:, n + 16, :] = ratio[64:128]

    half = lax.broadcasted_iota(jnp.int32, (32, 128), 1) < 64

    def decode_pair(c, h):
        def go(k, _):
            p = (2 * c + h) * PER + k
            rows = pl.ds(pl.multiple_of(32 * k, 32), 32)
            f0 = table[2 * p]
            f1 = table[2 * p + 1]
            for t in range(16):
                z, x = t // 4, t % 4
                one, two = ((z, x), (x, z))[h]
                left, right = 8 * z + x, 8 * z + 4 + x
                columns = slice(128 * t, 128 * t + 128)
                a = recv[h, c, 2 * one, two, rows, :].astype(jnp.float32)
                b = recv[h, c, 2 * one + 1, two, rows, :].astype(jnp.float32)
                for e, f, u in (
                    (0, f0, jnp.where(half, a, pltpu.roll(b, 64, 1))),
                    (1, f1, jnp.where(half, pltpu.roll(a, 64, 1), b)),
                ):
                    g = jnp.where(
                        half,
                        jnp.broadcast_to(f[:, left : left + 1], (32, 128)),
                        jnp.broadcast_to(f[:, right : right + 1], (32, 128)),
                    )
                    m = jnp.exp(jnp.log(jnp.abs(u)) * (1.0 / POWER))
                    v = jnp.where(u < 0.0, -m, m) * g
                    out[2 * p + e, :, columns] = v.astype(jnp.bfloat16)
            return 0

        return go

    def decode(c):
        for h in range(2):
            wait(recv.at[h, c, pl.ds(0, 7)], recv_sem.at[h, c])
            lax.fori_loop(0, PER, decode_pair(c, h), 0)

    wait(parts.at[0, three], parts_recv_sem.at[1])
    put(parts.at[mc], parts.at[mc], parts_send_sem.at[2], parts_recv_sem.at[2], mz, mx, mate)

    def step(c, _):
        go_on(c)

        @pl.when(c < CHUNKS - 2)
        def _():
            code(c + 2)
            leave(c + 2)

        decode(c - 1)
        return 0

    lax.fori_loop(1, CHUNKS - 1, step, 0)

    wait(parts.at[0], parts_recv_sem.at[2])
    mine = pl.ds(pl.multiple_of(16 * bank, 16), 16)
    low = half[0:8]
    for t in range(16):
        z, x = t // 4, t % 4
        a = parts[0, z, x].astype(jnp.float32)
        b = parts[1, z, x].astype(jnp.float32)
        block = jnp.concatenate(
            [
                jnp.where(low, a, pltpu.roll(b, 64, 1)),
                jnp.where(low, pltpu.roll(a, 64, 1), b),
            ],
            axis=0,
        )
        router[mine, 128 * t : 128 * t + 128] = block.astype(jnp.bfloat16)
    for i in range(1, 4):
        pltpu.make_async_remote_copy(
            src_ref=router.at[mine],
            dst_ref=router.at[mine],
            send_sem=row_send_sem,
            recv_sem=row_recv_sem,
            device_id={"bank": turn(bank, i)},
            device_id_type=MESH,
        ).start()

    go_on(CHUNKS - 1)
    decode(CHUNKS - 2)
    rest = pl.ds(0, 48)
    wait(router.at[rest], row_recv_sem)
    wait(router.at[rest], row_send_sem)
    wait(parts.at[0, 0, three], parts_send_sem.at[0])
    wait(parts.at[0, three], parts_send_sem.at[1])
    wait(parts.at[0], parts_send_sem.at[2])
    wait(sums_send.at[three], sums_send_sem)
    wait(sums_recv.at[pl.ds(0, 7)], sums_pass_sem)
    every = pl.ds(0, CHUNKS)
    both = pl.ds(0, 2)
    wait(send.at[both, every, three], send_sem)
    decode(CHUNKS - 1)
    wait(recv.at[both, every, pl.ds(0, 7)], pass_sem)


def hand_out(out, scale, router, gate, up, down, sg, su, sd, served, sem):
    copies = [pltpu.make_async_copy(router, served, sem.at[0])]
    for a, (big, small) in enumerate(((gate, sg), (up, su), (down, sd))):
        part = pl.ds(16 * a, 16)
        copies.append(pltpu.make_async_copy(out.at[part], big, sem.at[2 * a + 1]))
        copies.append(pltpu.make_async_copy(scale.at[part], small, sem.at[2 * a + 2]))
    for copy in copies:
        copy.start()
    for copy in copies:
        copy.wait()


def body(gate, up, down, weight, gain):
    vmem = pl.BlockSpec(memory_space=pltpu.VMEM)
    hbm = pl.BlockSpec(memory_space=pltpu.HBM)
    f32, bf16 = jnp.float32, jnp.bfloat16
    dma = pltpu.SemaphoreType.DMA
    out, scale, router = pl.pallas_call(
        exchange,
        name="exchange",
        out_shape=(
            pltpu.VMEM((48, 32, 2048), bf16),
            pltpu.VMEM((48, 32), f32),
            pltpu.VMEM((64, 2048), bf16),
        ),
        in_specs=[hbm, hbm, hbm, vmem, vmem],
        out_specs=(vmem, vmem, vmem),
        scratch_shapes=[
            pltpu.VMEM((48, 64, 1024), f32),
            pltpu.VMEM((2, CHUNKS, 4, 8, ROWS, 128), bf16),
            pltpu.VMEM((2, CHUNKS, 4, 8, ROWS, 128), bf16),
            pltpu.VMEM((2, CHUNKS, 8, 4, ROWS, 128), bf16),
            pltpu.VMEM((48, 1, 1024), f32),
            pltpu.VMEM((4, 8, 16, 128), f32),
            pltpu.VMEM((4, 8, 16, 128), f32),
            pltpu.VMEM((8, 4, 16, 128), f32),
            pltpu.VMEM((64, 32, 128), f32),
            pltpu.VMEM((2, 4, 4, 8, 128), bf16),
            dma((6,)),
            dma,
            dma((2, CHUNKS)),
            dma,
            dma((2, CHUNKS)),
            dma,
            dma,
            dma,
            dma,
            dma((3,)),
            dma((3,)),
            dma,
            dma,
        ],
        compiler_params=pltpu.CompilerParams(
            collective_id=0, has_side_effects=True, vmem_limit_bytes=48 * 2**20
        ),
    )(gate, up, jnp.swapaxes(down, 1, 2), weight.T, gain.reshape(1, 64))
    half = jax.ShapeDtypeStruct((16, 32, 2048), bf16)
    few = jax.ShapeDtypeStruct((16, 32), f32)
    gate, up, down, sg, su, sd, served = pl.pallas_call(
        hand_out,
        name="hand_out",
        out_shape=(half, half, half, few, few, few, jax.ShapeDtypeStruct((64, 2048), bf16)),
        in_specs=[vmem] * 3,
        out_specs=(hbm,) * 7,
        scratch_shapes=[dma((7,))],
        compiler_params=pltpu.CompilerParams(vmem_limit_bytes=16 * 2**20),
    )(*(pltpu.with_memory_space_constraint(a, pltpu.VMEM) for a in (out, scale, router)))
    return (
        jnp.swapaxes(gate, 1, 2),
        jnp.swapaxes(up, 1, 2),
        down,
        sg,
        su,
        sd,
        served.T,
    )


def solution(mesh):
    return jax.shard_map(
        body,
        mesh=mesh,
        in_specs=(
            P("bank", "zero", None),
            P("bank", "zero", None),
            P("bank", None, "zero"),
            P("zero", "bank"),
            P("zero"),
        ),
        out_specs=(
            P("bank", None, "zero"),
            P("bank", None, "zero"),
            P("bank", "zero", None),
            P("bank", "zero"),
            P("bank", "zero"),
            P("bank", "zero"),
            P(),
        ),
        check_vma=False,
    )
```

time: 92.4 us -> 86.6 us (0.937)
  the two profiles are of different devices: /device:TPU:3 before, /device:TPU:1 now
where the time goes in v3:
time: 86.6 us; the launch traced here: 86.4 us
  Pallas kernels  85.8 us (99%)
    pallas_call x1, Pallas kernels, body(): pl.pallas_call(exchange, name='exchange', out_shape=(pltpu.VMEM((48, 32,...  82.9 us
    pallas_call x1, Pallas kernels, body(): pl.pallas_call(hand_out, name='hand_out', out_shape=(half, half, half, fe...  2.86 us

profile of v3, /device:TPU:1, one launch (start us, length us, event | category | flops | bytes accessed | tf_op | source)
XLA Modules:
  0.0 86.4 jit_solution(16686243837663745818)
XLA Ops:
  0.6 82.9 %exchange.1 = (bf16[48,32,2048]{2,1,0:T(8,128)(2,1)S(1)}, f32[48,32]{1,0:T(8,128)S(1)}, bf16[64,2048]{1,0:T(8,128)(2,1)S(1)}) custom-call(f32[16,64,1024]{2,1,0:T(8,128)} %gate.1, f32[16,64,1024]{2,1,0:T(8,128)} %up.1, f32[16,64,1024]{2,1,0:T(8,128)} %bitcast.6, f32[16,64]{1,0:T(8,128)} %bitcast.7, f32[1,64]{1,0:T(1,128)} %bitcast.8), custom_call_target="tpu_custom_call" | custom-call | tf_op jit(solution)/shard_map/exchange/pallas_call | solution.py:310
  83.6 2.9 %hand_out.1 = (bf16[16,32,2048]{2,1,0:T(8,128)(2,1)}, bf16[16,32,2048]{2,1,0:T(8,128)(2,1)}, bf16[16,32,2048]{2,1,0:T(8,128)(2,1)}, f32[16,32]{1,0:T(8,128)}, f3...) custom-call(bf16[48,32,2048]{2,1,0:T(8,128)(2,1)S(1)} %get-tuple-element.17.out, ...), custom_call_target="tpu_custom_call" | custom-call | tf_op jit(solution)/shard_map/hand_out/pallas_call | solution.py:351

commit v4 on v3

--- a/solution.py
+++ b/solution.py
@@ -6,7 +6,9 @@
 from jax.sharding import PartitionSpec as P
 
 MESH = pl.DeviceIdType.MESH
-CHUNKS = 6
+CHUNKS = 12
+AHEAD = 4
+LOAD = 4
 PAIRS = 24
 PER = PAIRS // CHUNKS // 2
 ROWS = PER * 32
@@ -46,16 +48,15 @@
     def wait(ref, sem):
         pltpu.make_async_copy(ref, ref, sem).wait()
 
-    loads = []
-    for a, ref in enumerate((gate, up, down)):
-        for h in range(2):
-            copy = pltpu.make_async_copy(
-                ref.at[pl.ds(8 * h, 8)],
-                xin.at[pl.ds(16 * a + 8 * h, 8)],
-                in_sem.at[2 * a + h],
-            )
-            copy.start()
-            loads.append(copy)
+    loads = [
+        pltpu.make_async_copy(
+            ref.at[pl.ds(k, LOAD)], xin.at[pl.ds(16 * a + k, LOAD)], in_sem.at[4 * a + k // LOAD]
+        )
+        for a, ref in enumerate((gate, up, down))
+        for k in range(0, 16, LOAD)
+    ]
+    for copy in loads[:2]:
+        copy.start()
 
     barrier = pltpu.get_barrier_semaphore()
 
@@ -134,14 +135,20 @@
         recv[1, c, at_x] = relay[1, c, :, at_x]
 
     loads[0].wait()
-    lax.fori_loop(0, 8, add_up, 0)
+    for copy in loads[2:]:
+        copy.start()
+    lax.fori_loop(0, LOAD, add_up, 0)
     code(0)
     pl.semaphore_wait(barrier, 16)
     leave(0)
-
-    for i in range(1, 6):
+    loads[1].wait()
+    lax.fori_loop(LOAD, 2 * LOAD, add_up, 0)
+    code(1)
+    leave(1)
+
+    for i in range(2, 12):
         loads[i].wait()
-        lax.fori_loop(8 * i, 8 * i + 8, add_up, 0)
+        lax.fori_loop(LOAD * i, LOAD * i + LOAD, add_up, 0)
 
     pad = jnp.zeros((16, 128), jnp.float32)
     for b in range(8):
@@ -156,8 +163,13 @@
         put(parts.at[mc, mz, mx], parts.at[mc, mz, mx], parts_send_sem.at[0], parts_recv_sem.at[0], mz, x, mc)
     sums_relay[mx] = sums_send[mx]
 
-    code(1)
-    leave(1)
+    def code_and_leave(c, _):
+        code(c)
+        leave(c)
+        return 0
+
+    lax.fori_loop(2, AHEAD, code_and_leave, 0)
+    go_on(0)
 
     wait(sums_relay.at[three], sums_relay_sem)
     wait(parts.at[0, 0, three], parts_recv_sem.at[0])
@@ -170,9 +182,9 @@
     put(sums_relay.at[four, 2 * mz + mate], sums_recv.at[at_z], sums_pass_sem, sums_recv_sem, mz, mx, mate)
     sums_recv[at_z] = sums_relay[:, at_z]
 
-    go_on(0)
-    code(2)
-    leave(2)
+    code_and_leave(AHEAD, 0)
+    go_on(1)
+    code_and_leave(AHEAD + 1, 0)
 
     wait(sums_recv.at[pl.ds(0, 7)], sums_recv_sem)
     total = jnp.zeros((16, 128), jnp.float32)
@@ -235,45 +247,49 @@
     wait(parts.at[0, three], parts_recv_sem.at[1])
     put(parts.at[mc], parts.at[mc], parts_send_sem.at[2], parts_recv_sem.at[2], mz, mx, mate)
 
+    mine = pl.ds(pl.multiple_of(16 * bank, 16), 16)
+
+    def serve_rows():
+        wait(parts.at[0], parts_recv_sem.at[2])
+        low = half[0:8]
+        for t in range(16):
+            z, x = t // 4, t % 4
+            a = parts[0, z, x].astype(jnp.float32)
+            b = parts[1, z, x].astype(jnp.float32)
+            block = jnp.concatenate(
+                [
+                    jnp.where(low, a, pltpu.roll(b, 64, 1)),
+                    jnp.where(low, pltpu.roll(a, 64, 1), b),
+                ],
+                axis=0,
+            )
+            router[mine, 128 * t : 128 * t + 128] = block.astype(jnp.bfloat16)
+        for i in range(1, 4):
+            pltpu.make_async_remote_copy(
+                src_ref=router.at[mine],
+                dst_ref=router.at[mine],
+                send_sem=row_send_sem,
+                recv_sem=row_recv_sem,
+                device_id={"bank": turn(bank, i)},
+                device_id_type=MESH,
+            ).start()
+
     def step(c, _):
         go_on(c)
 
-        @pl.when(c < CHUNKS - 2)
+        @pl.when(c < CHUNKS - AHEAD)
         def _():
-            code(c + 2)
-            leave(c + 2)
-
-        decode(c - 1)
+            code_and_leave(c + AHEAD, 0)
+
+        decode(c - 2)
+
+        @pl.when(c == CHUNKS // 2)
+        def _():
+            serve_rows()
+
         return 0
 
-    lax.fori_loop(1, CHUNKS - 1, step, 0)
-
-    wait(parts.at[0], parts_recv_sem.at[2])
-    mine = pl.ds(pl.multiple_of(16 * bank, 16), 16)
-    low = half[0:8]
-    for t in range(16):
-        z, x = t // 4, t % 4
-        a = parts[0, z, x].astype(jnp.float32)
-        b = parts[1, z, x].astype(jnp.float32)
-        block = jnp.concatenate(
-            [
-                jnp.where(low, a, pltpu.roll(b, 64, 1)),
-                jnp.where(low, pltpu.roll(a, 64, 1), b),
-            ],
-            axis=0,
-        )
-        router[mine, 128 * t : 128 * t + 128] = block.astype(jnp.bfloat16)
-    for i in range(1, 4):
-        pltpu.make_async_remote_copy(
-            src_ref=router.at[mine],
-            dst_ref=router.at[mine],
-            send_sem=row_send_sem,
-            recv_sem=row_recv_sem,
-            device_id={"bank": turn(bank, i)},
-            device_id_type=MESH,
-        ).start()
-
-    go_on(CHUNKS - 1)
+    lax.fori_loop(2, CHUNKS, step, 0)
     decode(CHUNKS - 2)
     rest = pl.ds(0, 48)
     wait(router.at[rest], row_recv_sem)
@@ -328,7 +344,7 @@
             pltpu.VMEM((8, 4, 16, 128), f32),
             pltpu.VMEM((64, 32, 128), f32),
             pltpu.VMEM((2, 4, 4, 8, 128), bf16),
-            dma((6,)),
+            dma((12,)),
             dma,
             dma((2, CHUNKS)),
             dma,

time: 86.6 us -> 85.5 us (0.987)
  Pallas kernels: 85.8 us -> 84.7 us
    pallas_call x1, Pallas kernels: 82.9 us -> 81.9 us  [body(): pl.pallas_call(exchange, name='exchange', out_shape=(pltpu.VMEM((48, 32,...]
where the time goes in v4:
time: 85.5 us; the launch traced here: 85.4 us
  Pallas kernels  84.7 us (99%)
    pallas_call x1, Pallas kernels, body(): pl.pallas_call(exchange, name='exchange', out_shape=(pltpu.VMEM((48, 32,...  81.9 us
    pallas_call x1, Pallas kernels, body(): pl.pallas_call(hand_out, name='hand_out', out_shape=(half, half, half, fe...  2.86 us

profile of v4, /device:TPU:1, one launch (start us, length us, event | category | flops | bytes accessed | tf_op | source)
XLA Modules:
  0.0 85.4 jit_solution(3750888585113887322)
XLA Ops:
  0.6 81.9 %exchange.1 = (bf16[48,32,2048]{2,1,0:T(8,128)(2,1)S(1)}, f32[48,32]{1,0:T(8,128)S(1)}, bf16[64,2048]{1,0:T(8,128)(2,1)S(1)}) custom-call(f32[16,64,1024]{2,1,0:T(8,128)} %gate.1, f32[16,64,1024]{2,1,0:T(8,128)} %up.1, f32[16,64,1024]{2,1,0:T(8,128)} %bitcast.6, f32[16,64]{1,0:T(8,128)} %bitcast.7, f32[1,64]{1,0:T(1,128)} %bitcast.8), custom_call_target="tpu_custom_call" | custom-call | tf_op jit(solution)/shard_map/exchange/pallas_call | solution.py:326
  82.5 2.9 %hand_out.1 = (bf16[16,32,2048]{2,1,0:T(8,128)(2,1)}, bf16[16,32,2048]{2,1,0:T(8,128)(2,1)}, bf16[16,32,2048]{2,1,0:T(8,128)(2,1)}, f32[16,32]{1,0:T(8,128)}, f3...) custom-call(bf16[48,32,2048]{2,1,0:T(8,128)(2,1)S(1)} %get-tuple-element.17.out, ...), custom_call_target="tpu_custom_call" | custom-call | tf_op jit(solution)/shard_map/hand_out/pallas_call | solution.py:367

commit v5 on v4

--- a/solution.py
+++ b/solution.py
@@ -16,10 +16,41 @@
 UP = 2.0**6.25
 
 
+def left_half():
+    return lax.broadcasted_iota(jnp.int32, (32, 128), 1) < 64
+
+
+def decode_pair(recv, table, out, c, h, k, place):
+    half = left_half()
+    p = (2 * c + h) * PER + k
+    rows = pl.ds(pl.multiple_of(32 * k, 32), 32)
+    f0 = table[2 * p]
+    f1 = table[2 * p + 1]
+    for t in range(16):
+        z, x = t // 4, t % 4
+        one, two = ((z, x), (x, z))[h]
+        left, right = 8 * z + x, 8 * z + 4 + x
+        columns = slice(128 * t, 128 * t + 128)
+        a = recv[h, c, 2 * one, two, rows, :].astype(jnp.float32)
+        b = recv[h, c, 2 * one + 1, two, rows, :].astype(jnp.float32)
+        for e, f, u in (
+            (0, f0, jnp.where(half, a, pltpu.roll(b, 64, 1))),
+            (1, f1, jnp.where(half, pltpu.roll(a, 64, 1), b)),
+        ):
+            g = jnp.where(
+                half,
+                jnp.broadcast_to(f[:, left : left + 1], (32, 128)),
+                jnp.broadcast_to(f[:, right : right + 1], (32, 128)),
+            )
+            m = jnp.exp(jnp.log(jnp.abs(u)) * (1.0 / POWER))
+            v = jnp.where(u < 0.0, -m, m) * g
+            out[2 * place + e, :, columns] = v.astype(jnp.bfloat16)
+
+
 def exchange(
     gate, up, down, weight, gain,
-    out, scale, router,
-    xin, send, relay, recv, sums, sums_send, sums_relay, sums_recv, table, parts,
+    out, scale, router, recv, table,
+    xin, send, relay, sums, sums_send, sums_relay, sums_recv, parts,
     in_sem, send_sem, relay_sem, pass_sem, recv_sem,
     sums_send_sem, sums_relay_sem, sums_pass_sem, sums_recv_sem,
     parts_send_sem, parts_recv_sem, row_send_sem, row_recv_sem,
@@ -208,41 +239,17 @@
         table[:, n, :] = ratio[0:64]
         table[:, n + 16, :] = ratio[64:128]
 
-    half = lax.broadcasted_iota(jnp.int32, (32, 128), 1) < 64
-
-    def decode_pair(c, h):
-        def go(k, _):
-            p = (2 * c + h) * PER + k
-            rows = pl.ds(pl.multiple_of(32 * k, 32), 32)
-            f0 = table[2 * p]
-            f1 = table[2 * p + 1]
-            for t in range(16):
-                z, x = t // 4, t % 4
-                one, two = ((z, x), (x, z))[h]
-                left, right = 8 * z + x, 8 * z + 4 + x
-                columns = slice(128 * t, 128 * t + 128)
-                a = recv[h, c, 2 * one, two, rows, :].astype(jnp.float32)
-                b = recv[h, c, 2 * one + 1, two, rows, :].astype(jnp.float32)
-                for e, f, u in (
-                    (0, f0, jnp.where(half, a, pltpu.roll(b, 64, 1))),
-                    (1, f1, jnp.where(half, pltpu.roll(a, 64, 1), b)),
-                ):
-                    g = jnp.where(
-                        half,
-                        jnp.broadcast_to(f[:, left : left + 1], (32, 128)),
-                        jnp.broadcast_to(f[:, right : right + 1], (32, 128)),
-                    )
-                    m = jnp.exp(jnp.log(jnp.abs(u)) * (1.0 / POWER))
-                    v = jnp.where(u < 0.0, -m, m) * g
-                    out[2 * p + e, :, columns] = v.astype(jnp.bfloat16)
-            return 0
-
-        return go
+    half = left_half()
 
     def decode(c):
         for h in range(2):
             wait(recv.at[h, c, pl.ds(0, 7)], recv_sem.at[h, c])
-            lax.fori_loop(0, PER, decode_pair(c, h), 0)
+
+            def go(k, _):
+                decode_pair(recv, table, out, c, h, k, (2 * c + h) * PER + k)
+                return 0
+
+            lax.fori_loop(0, PER, go, 0)
 
     wait(parts.at[0, three], parts_recv_sem.at[1])
     put(parts.at[mc], parts.at[mc], parts_send_sem.at[2], parts_recv_sem.at[2], mz, mx, mate)
@@ -302,20 +309,39 @@
     every = pl.ds(0, CHUNKS)
     both = pl.ds(0, 2)
     wait(send.at[both, every, three], send_sem)
-    decode(CHUNKS - 1)
+    for h in range(2):
+        wait(recv.at[h, CHUNKS - 1, pl.ds(0, 7)], recv_sem.at[h, CHUNKS - 1])
     wait(recv.at[both, every, pl.ds(0, 7)], pass_sem)
 
 
-def hand_out(out, scale, router, gate, up, down, sg, su, sd, served, sem):
-    copies = [pltpu.make_async_copy(router, served, sem.at[0])]
+def hand_out(
+    out, scale, router, recv, table,
+    gate, up, down, sg, su, sd, served,
+    last, sem,
+):
+    few = 4 * PER
+    copies = []
+
+    def copy(src, dst):
+        copies.append(pltpu.make_async_copy(src, dst, sem.at[len(copies)]))
+        copies[-1].start()
+
     for a, (big, small) in enumerate(((gate, sg), (up, su), (down, sd))):
-        part = pl.ds(16 * a, 16)
-        copies.append(pltpu.make_async_copy(out.at[part], big, sem.at[2 * a + 1]))
-        copies.append(pltpu.make_async_copy(scale.at[part], small, sem.at[2 * a + 2]))
-    for copy in copies:
-        copy.start()
-    for copy in copies:
-        copy.wait()
+        count = 16 - few * (a == 2)
+        copy(out.at[pl.ds(16 * a, count)], big.at[pl.ds(0, count)])
+        copy(scale.at[pl.ds(16 * a, 16)], small)
+    copy(router, served)
+    for h in range(2):
+
+        def go(k, _):
+            decode_pair(recv, table, last, CHUNKS - 1, h, k, h * PER + k)
+            return 0
+
+        lax.fori_loop(0, PER, go, 0)
+        part = 2 * PER
+        copy(last.at[pl.ds(part * h, part)], down.at[pl.ds(16 - few + part * h, part)])
+    for c in copies:
+        c.wait()
 
 
 def body(gate, up, down, weight, gain):
@@ -323,26 +349,26 @@
     hbm = pl.BlockSpec(memory_space=pltpu.HBM)
     f32, bf16 = jnp.float32, jnp.bfloat16
     dma = pltpu.SemaphoreType.DMA
-    out, scale, router = pl.pallas_call(
+    results = pl.pallas_call(
         exchange,
         name="exchange",
         out_shape=(
             pltpu.VMEM((48, 32, 2048), bf16),
             pltpu.VMEM((48, 32), f32),
             pltpu.VMEM((64, 2048), bf16),
+            pltpu.VMEM((2, CHUNKS, 8, 4, ROWS, 128), bf16),
+            pltpu.VMEM((64, 32, 128), f32),
         ),
         in_specs=[hbm, hbm, hbm, vmem, vmem],
-        out_specs=(vmem, vmem, vmem),
+        out_specs=(vmem,) * 5,
         scratch_shapes=[
             pltpu.VMEM((48, 64, 1024), f32),
             pltpu.VMEM((2, CHUNKS, 4, 8, ROWS, 128), bf16),
             pltpu.VMEM((2, CHUNKS, 4, 8, ROWS, 128), bf16),
-            pltpu.VMEM((2, CHUNKS, 8, 4, ROWS, 128), bf16),
             pltpu.VMEM((48, 1, 1024), f32),
             pltpu.VMEM((4, 8, 16, 128), f32),
             pltpu.VMEM((4, 8, 16, 128), f32),
             pltpu.VMEM((8, 4, 16, 128), f32),
-            pltpu.VMEM((64, 32, 128), f32),
             pltpu.VMEM((2, 4, 4, 8, 128), bf16),
             dma((12,)),
             dma,
@@ -359,7 +385,7 @@
             dma,
         ],
         compiler_params=pltpu.CompilerParams(
-            collective_id=0, has_side_effects=True, vmem_limit_bytes=48 * 2**20
+            collective_id=0, has_side_effects=True, vmem_limit_bytes=49 * 2**20
         ),
     )(gate, up, jnp.swapaxes(down, 1, 2), weight.T, gain.reshape(1, 64))
     half = jax.ShapeDtypeStruct((16, 32, 2048), bf16)
@@ -368,11 +394,11 @@
         hand_out,
         name="hand_out",
         out_shape=(half, half, half, few, few, few, jax.ShapeDtypeStruct((64, 2048), bf16)),
-        in_specs=[vmem] * 3,
+        in_specs=[vmem] * 5,
         out_specs=(hbm,) * 7,
-        scratch_shapes=[dma((7,))],
+        scratch_shapes=[pltpu.VMEM((4 * PER, 32, 2048), bf16), dma((9,))],
         compiler_params=pltpu.CompilerParams(vmem_limit_bytes=16 * 2**20),
-    )(*(pltpu.with_memory_space_constraint(a, pltpu.VMEM) for a in (out, scale, router)))
+    )(*(pltpu.with_memory_space_constraint(a, pltpu.VMEM) for a in results))
     return (
         jnp.swapaxes(gate, 1, 2),
         jnp.swapaxes(up, 1, 2),

time: 85.5 us -> 84.6 us (0.989)
  Pallas kernels: 84.7 us -> 83.8 us
    pallas_call x1, Pallas kernels: 81.9 us -> 80.9 us  [body(): pl.pallas_call(exchange, name='exchange', out_shape=(pltpu.VMEM((48, 32,...]
where the time goes in v5:
time: 84.6 us; the launch traced here: 84.4 us
  Pallas kernels  83.8 us (99%)
    pallas_call x1, Pallas kernels, body(): pl.pallas_call(exchange, name='exchange', out_shape=(pltpu.VMEM((48, 32,...  80.9 us
    pallas_call x1, Pallas kernels, body(): pl.pallas_call(hand_out, name='hand_out', out_shape=(half, half, half, fe...  2.81 us

profile of v5, /device:TPU:1, one launch (start us, length us, event | category | flops | bytes accessed | tf_op | source)
XLA Modules:
  0.0 84.4 jit_solution(8252138661656448087)
XLA Ops:
  0.6 80.9 %exchange.1 = (bf16[48,32,2048]{2,1,0:T(8,128)(2,1)S(1)}, f32[48,32]{1,0:T(8,128)S(1)}, bf16[64,2048]{1,0:T(8,128)(2,1)S(1)}, bf16[2,12,8,4,32,128]{5,4,3,2,1,0:T(8,128)(2,1)S(1)}, f32[64,32,128]{2,1,0:T(8,128)S(1)}) custom-call(f32[16,64,1024]{2,1,0:T(8,128)} %gate.1, f32[16,64,1024]{2,1,0:T(8,128)} %up.1, f32[16,64,1024]{2,1,0:T(8,128)} %bitcast.6, ...), custom_call_target="tpu_custom_call" | custom-call | tf_op jit(solution)/shard_map/exchange/pallas_call | solution.py:352
  81.6 2.8 %hand_out.1 = (bf16[16,32,2048]{2,1,0:T(8,128)(2,1)}, bf16[16,32,2048]{2,1,0:T(8,128)(2,1)}, bf16[16,32,2048]{2,1,0:T(8,128)(2,1)}, f32[16,32]{1,0:T(8,128)}, f3...) custom-call(bf16[48,32,2048]{2,1,0:T(8,128)(2,1)S(1)} %get-tuple-element.19.out, ...), custom_call_target="tpu_custom_call" | custom-call | tf_op jit(solution)/shard_map/hand_out/pallas_call | solution.py:393

commit v6 on v5

--- a/solution.py
+++ b/solution.py
@@ -20,12 +20,13 @@
     return lax.broadcasted_iota(jnp.int32, (32, 128), 1) < 64
 
 
-def decode_pair(recv, table, out, c, h, k, place):
+def decode_pair(recv, table, out, totals, wide, c, h, k, place):
     half = left_half()
     p = (2 * c + h) * PER + k
     rows = pl.ds(pl.multiple_of(32 * k, 32), 32)
     f0 = table[2 * p]
     f1 = table[2 * p + 1]
+    squares = [jnp.zeros((32, 128), jnp.float32)] * 2
     for t in range(16):
         z, x = t // 4, t % 4
         one, two = ((z, x), (x, z))[h]
@@ -44,13 +45,22 @@
             )
             m = jnp.exp(jnp.log(jnp.abs(u)) * (1.0 / POWER))
             v = jnp.where(u < 0.0, -m, m) * g
-            out[2 * place + e, :, columns] = v.astype(jnp.bfloat16)
+            wide[e, :, columns] = v
+            squares[e] = squares[e] + v * v
+    lane = lax.broadcasted_iota(jnp.int32, (32, 128), 1)
+    for e in range(2):
+        total = jnp.sum(squares[e], axis=1, keepdims=True)
+        totals[...] = jnp.where(lane == 2 * p + e, total, totals[...])
+        r = lax.rsqrt(total)
+        for t in range(16):
+            columns = slice(128 * t, 128 * t + 128)
+            out[2 * place + e, :, columns] = (wide[e, :, columns] * r).astype(jnp.bfloat16)
 
 
 def exchange(
     gate, up, down, weight, gain,
-    out, scale, router, recv, table,
-    xin, send, relay, sums, sums_send, sums_relay, sums_recv, parts,
+    out, totals, router, recv, table,
+    xin, send, relay, sums, sums_send, sums_relay, sums_recv, parts, wide_rows,
     in_sem, send_sem, relay_sem, pass_sem, recv_sem,
     sums_send_sem, sums_relay_sem, sums_pass_sem, sums_recv_sem,
     parts_send_sem, parts_recv_sem, row_send_sem, row_recv_sem,
@@ -108,7 +118,8 @@
 
     def add_up(e, _):
         x = xin[e]
-        sums[e] = jnp.sum(x * x, axis=0, keepdims=True)
+        norm = jnp.sqrt(jnp.sum(x * x, axis=0, keepdims=True))
+        sums[e] = norm.astype(jnp.bfloat16).astype(jnp.float32)
         return 0
 
     def code_pair(c, h):
@@ -120,7 +131,7 @@
                 halves = []
                 for e in range(2):
                     s = sums[2 * p + e, :, columns]
-                    r = jnp.where(s > 0.0, lax.rsqrt(s) * UP, 0.0)
+                    r = jnp.where(s > 0.0, UP / s, 0.0)
                     halves.append(xin[2 * p + e, :, columns] * r)
                 y = jnp.concatenate(halves, axis=0).T
                 y2 = y * y
@@ -187,7 +198,7 @@
         t = jnp.concatenate([s, pad, pltpu.roll(s, 112, 1), pad], axis=0).T
         for q in range(4):
             z, x, d = b // 2, b % 2 * 2 + q // 2, q % 2
-            sums_send[x, 2 * z + d] = t[32 * q : 32 * q + 16]
+            sums_send[x, 2 * z + d] = t[32 * q : 32 * q + 16].astype(jnp.bfloat16)
     for i in (1, 3, 2):
         x = turn(mx, i)
         put(sums_send.at[x], sums_relay.at[mx], sums_send_sem, sums_relay_sem, mz, x, mc)
@@ -218,26 +229,12 @@
     code_and_leave(AHEAD + 1, 0)
 
     wait(sums_recv.at[pl.ds(0, 7)], sums_recv_sem)
-    total = jnp.zeros((16, 128), jnp.float32)
-    for s in range(32):
-        total = total + sums_recv[s // 4, s % 4]
-    root = jnp.sqrt(jnp.concatenate([total] + [jnp.zeros((112, 128), jnp.float32)], 0).T)
-    first, second = root[0:48], pltpu.roll(root[64:112], 16, 1)
-    lane = lax.broadcasted_iota(jnp.int32, (48, 128), 1)
-    scale[...] = jnp.where(lane < 16, first, second)[:, 0:32]
-
+    wide = sums_recv[...].astype(jnp.float32).reshape(32, 16, 128)
     for n in range(16):
-        rows = jnp.concatenate(
-            [
-                sums_recv[:, :, n, :].reshape(32, 128),
-                jnp.zeros((96, 128), jnp.float32),
-            ],
-            axis=0,
-        ).T
-        whole = jnp.sum(rows, axis=1, keepdims=True)
-        ratio = jnp.sqrt(rows) * lax.rsqrt(whole) * (1.0 / UP)
-        table[:, n, :] = ratio[0:64]
-        table[:, n + 16, :] = ratio[64:128]
+        rows = jnp.concatenate([wide[:, n, :], jnp.zeros((96, 128), jnp.float32)], axis=0).T
+        table[:, n, :] = rows[0:64] * (1.0 / UP)
+        table[:, n + 16, :] = rows[64:128] * (1.0 / UP)
+    totals[...] = jnp.zeros_like(totals)
 
     half = left_half()
 
@@ -246,7 +243,7 @@
             wait(recv.at[h, c, pl.ds(0, 7)], recv_sem.at[h, c])
 
             def go(k, _):
-                decode_pair(recv, table, out, c, h, k, (2 * c + h) * PER + k)
+                decode_pair(recv, table, out, totals, wide_rows, c, h, k, (2 * c + h) * PER + k)
                 return 0
 
             lax.fori_loop(0, PER, go, 0)
@@ -315,9 +312,9 @@
 
 
 def hand_out(
-    out, scale, router, recv, table,
+    out, begun, router, recv, table,
     gate, up, down, sg, su, sd, served,
-    last, sem,
+    last, totals, scale, wide_rows, sem,
 ):
     few = 4 * PER
     copies = []
@@ -326,20 +323,24 @@
         copies.append(pltpu.make_async_copy(src, dst, sem.at[len(copies)]))
         copies[-1].start()
 
-    for a, (big, small) in enumerate(((gate, sg), (up, su), (down, sd))):
+    for a, big in enumerate((gate, up, down)):
         count = 16 - few * (a == 2)
         copy(out.at[pl.ds(16 * a, count)], big.at[pl.ds(0, count)])
-        copy(scale.at[pl.ds(16 * a, 16)], small)
     copy(router, served)
+    totals[...] = begun[...]
     for h in range(2):
 
         def go(k, _):
-            decode_pair(recv, table, last, CHUNKS - 1, h, k, h * PER + k)
+            decode_pair(recv, table, last, totals, wide_rows, CHUNKS - 1, h, k, h * PER + k)
             return 0
 
         lax.fori_loop(0, PER, go, 0)
         part = 2 * PER
         copy(last.at[pl.ds(part * h, part)], down.at[pl.ds(16 - few + part * h, part)])
+    turned = jnp.concatenate([totals[...], jnp.zeros((96, 128), jnp.float32)], axis=0).T
+    scale[...] = jnp.sqrt(turned[0:48, 0:32])
+    for a, small in enumerate((sg, su, sd)):
+        copy(scale.at[pl.ds(16 * a, 16)], small)
     for c in copies:
         c.wait()
 
@@ -354,7 +355,7 @@
         name="exchange",
         out_shape=(
             pltpu.VMEM((48, 32, 2048), bf16),
-            pltpu.VMEM((48, 32), f32),
+            pltpu.VMEM((32, 128), f32),
             pltpu.VMEM((64, 2048), bf16),
             pltpu.VMEM((2, CHUNKS, 8, 4, ROWS, 128), bf16),
             pltpu.VMEM((64, 32, 128), f32),
@@ -366,10 +367,11 @@
             pltpu.VMEM((2, CHUNKS, 4, 8, ROWS, 128), bf16),
             pltpu.VMEM((2, CHUNKS, 4, 8, ROWS, 128), bf16),
             pltpu.VMEM((48, 1, 1024), f32),
-            pltpu.VMEM((4, 8, 16, 128), f32),
-            pltpu.VMEM((4, 8, 16, 128), f32),
-            pltpu.VMEM((8, 4, 16, 128), f32),
+            pltpu.VMEM((4, 8, 16, 128), bf16),
+            pltpu.VMEM((4, 8, 16, 128), bf16),
+            pltpu.VMEM((8, 4, 16, 128), bf16),
             pltpu.VMEM((2, 4, 4, 8, 128), bf16),
+            pltpu.VMEM((2, 32, 2048), f32),
             dma((12,)),
             dma,
             dma((2, CHUNKS)),
@@ -396,7 +398,13 @@
         out_shape=(half, half, half, few, few, few, jax.ShapeDtypeStruct((64, 2048), bf16)),
         in_specs=[vmem] * 5,
         out_specs=(hbm,) * 7,
-        scratch_shapes=[pltpu.VMEM((4 * PER, 32, 2048), bf16), dma((9,))],
+        scratch_shapes=[
+            pltpu.VMEM((4 * PER, 32, 2048), bf16),
+            pltpu.VMEM((32, 128), f32),
+            pltpu.VMEM((48, 32), f32),
+            pltpu.VMEM((2, 32, 2048), f32),
+            dma((9,)),
+        ],
         compiler_params=pltpu.CompilerParams(vmem_limit_bytes=16 * 2**20),
     )(*(pltpu.with_memory_space_constraint(a, pltpu.VMEM) for a in results))
     return (

time: 84.6 us -> 83.7 us (0.989)
  Pallas kernels: 83.8 us -> 82.8 us
    pallas_call x1, Pallas kernels: 80.9 us -> 79.8 us  [body(): pl.pallas_call(exchange, name='exchange', out_shape=(pltpu.VMEM((48, 32,...]
where the time goes in v6:
time: 83.7 us; the launch traced here: 83.5 us
  Pallas kernels  82.8 us (99%)
    pallas_call x1, Pallas kernels, body(): pl.pallas_call(exchange, name='exchange', out_shape=(pltpu.VMEM((48, 32,...  79.8 us
    pallas_call x1, Pallas kernels, body(): pl.pallas_call(hand_out, name='hand_out', out_shape=(half, half, half, fe...  3.1 us

profile of v6, /device:TPU:1, one launch (start us, length us, event | category | flops | bytes accessed | tf_op | source)
XLA Modules:
  0.0 83.5 jit_solution(15521983787650895421)
XLA Ops:
  0.6 79.8 %exchange.1 = (bf16[48,32,2048]{2,1,0:T(8,128)(2,1)S(1)}, f32[32,128]{1,0:T(8,128)S(1)}, bf16[64,2048]{1,0:T(8,128)(2,1)S(1)}, bf16[2,12,8,4,32,128]{5,4,3,2,1,0:T(8,128)(2,1)S(1)}, f32[64,32,128]{2,1,0:T(8,128)S(1)}) custom-call(f32[16,64,1024]{2,1,0:T(8,128)} %gate.1, f32[16,64,1024]{2,1,0:T(8,128)} %up.1, f32[16,64,1024]{2,1,0:T(8,128)} %bitcast.6, ...), custom_call_target="tpu_custom_call" | custom-call | tf_op jit(solution)/shard_map/exchange/pallas_call | solution.py:353
  80.4 3.1 %hand_out.1 = (bf16[16,32,2048]{2,1,0:T(8,128)(2,1)}, bf16[16,32,2048]{2,1,0:T(8,128)(2,1)}, bf16[16,32,2048]{2,1,0:T(8,128)(2,1)}, f32[16,32]{1,0:T(8,128)}, f3...) custom-call(bf16[48,32,2048]{2,1,0:T(8,128)(2,1)S(1)} %get-tuple-element.19.out, ...), custom_call_target="tpu_custom_call" | custom-call | tf_op jit(solution)/shard_map/hand_out/pallas_call | solution.py:395

commit v7 on v6

--- a/solution.py
+++ b/solution.py
@@ -8,32 +8,32 @@
 MESH = pl.DeviceIdType.MESH
 CHUNKS = 12
 AHEAD = 4
-LOAD = 4
 PAIRS = 24
-PER = PAIRS // CHUNKS // 2
-ROWS = PER * 32
 POWER = 20
 UP = 2.0**6.25
 
 
+def turned(h, a, b):
+    return a + h * (b - a), b + h * (a - b)
+
+
 def left_half():
     return lax.broadcasted_iota(jnp.int32, (32, 128), 1) < 64
 
 
-def decode_pair(recv, table, out, totals, wide, c, h, k, place):
+def decode_pair(recv, table, out, totals, wide, p, place):
     half = left_half()
-    p = (2 * c + h) * PER + k
-    rows = pl.ds(pl.multiple_of(32 * k, 32), 32)
+    h = lax.rem(p, 2)
     f0 = table[2 * p]
     f1 = table[2 * p + 1]
     squares = [jnp.zeros((32, 128), jnp.float32)] * 2
     for t in range(16):
         z, x = t // 4, t % 4
-        one, two = ((z, x), (x, z))[h]
+        one, two = turned(h, z, x)
         left, right = 8 * z + x, 8 * z + 4 + x
         columns = slice(128 * t, 128 * t + 128)
-        a = recv[h, c, 2 * one, two, rows, :].astype(jnp.float32)
-        b = recv[h, c, 2 * one + 1, two, rows, :].astype(jnp.float32)
+        a = recv[p, 2 * one, two].astype(jnp.float32)
+        b = recv[p, 2 * one + 1, two].astype(jnp.float32)
         for e, f, u in (
             (0, f0, jnp.where(half, a, pltpu.roll(b, 64, 1))),
             (1, f1, jnp.where(half, pltpu.roll(a, 64, 1), b)),
@@ -91,10 +91,9 @@
 
     loads = [
         pltpu.make_async_copy(
-            ref.at[pl.ds(k, LOAD)], xin.at[pl.ds(16 * a + k, LOAD)], in_sem.at[4 * a + k // LOAD]
+            ref.at[pl.ds(k, count)], xin.at[pl.ds(16 * a + k, count)], in_sem.at[i]
         )
-        for a, ref in enumerate((gate, up, down))
-        for k in range(0, 16, LOAD)
+        for i, (a, ref, k, count) in enumerate(((0, gate, 0, 4), (0, gate, 4, 4), (0, gate, 8, 8), (1, up, 0, 16), (2, down, 0, 16)))
     ]
     for copy in loads[:2]:
         copy.start()
@@ -122,75 +121,76 @@
         sums[e] = norm.astype(jnp.bfloat16).astype(jnp.float32)
         return 0
 
-    def code_pair(c, h):
-        def go(k, _):
-            p = (2 * c + h) * PER + k
-            rows = pl.ds(pl.multiple_of(32 * k, 32), 32)
-            for b in range(8):
-                columns = slice(128 * b, 128 * b + 128)
-                halves = []
-                for e in range(2):
-                    s = sums[2 * p + e, :, columns]
-                    r = jnp.where(s > 0.0, UP / s, 0.0)
-                    halves.append(xin[2 * p + e, :, columns] * r)
-                y = jnp.concatenate(halves, axis=0).T
-                y2 = y * y
-                y4 = y2 * y2
-                y8 = y4 * y4
-                y20 = y8 * y8 * y4
-                u = jnp.where(y < 0.0, -y20, y20).astype(jnp.bfloat16)
-                for q in range(4):
-                    z, x, d = b // 2, b % 2 * 2 + q // 2, q % 2
-                    first, second = ((x, z), (z, x))[h]
-                    send[h, c, first, 2 * second + d, rows, :] = u[32 * q : 32 * q + 32]
-            return 0
-
-        return go
-
-    def code(c):
-        for h in range(2):
-            lax.fori_loop(0, PER, code_pair(c, h), 0)
-
-    def leave(c):
-        for i in (1, 3, 2):
-            x, z = turn(mx, i), turn(mz, i)
-            put(send.at[0, c, x], relay.at[0, c, mx], send_sem, relay_sem.at[0, c], mz, x, mc)
-            put(send.at[1, c, z], relay.at[1, c, mz], send_sem, relay_sem.at[1, c], z, mx, mc)
-        relay[0, c, mx] = send[0, c, mx]
-        relay[1, c, mz] = send[1, c, mz]
+    def code(p):
+        h = lax.rem(p, 2)
+        for b in range(8):
+            columns = slice(128 * b, 128 * b + 128)
+            halves = []
+            for e in range(2):
+                s = sums[2 * p + e, :, columns]
+                r = jnp.where(s > 0.0, UP / s, 0.0)
+                halves.append(xin[2 * p + e, :, columns] * r)
+            y = jnp.concatenate(halves, axis=0).T
+            y2 = y * y
+            y4 = y2 * y2
+            y8 = y4 * y4
+            y20 = y8 * y8 * y4
+            u = jnp.where(y < 0.0, -y20, y20).astype(jnp.bfloat16)
+            for q in range(4):
+                z, x, d = b // 2, b % 2 * 2 + q // 2, q % 2
+                first, second = turned(h, x, z)
+                send[p, first, 2 * second + d] = u[32 * q : 32 * q + 32]
+
+    def leave(p):
+        h = lax.rem(p, 2)
+        mine, other = turned(h, mx, mz)
+        for i in (2, 1, 3):
+            to = turn(mine, i)
+            x, z = turned(h, to, other)
+            put(send.at[p, to], relay.at[p, mine], send_sem, relay_sem.at[p], z, x, mc)
+        relay[p, mine] = send[p, mine]
 
     four = pl.ds(0, 4)
     three = pl.ds(0, 3)
 
-    def go_on(c):
-        for h in range(2):
-            wait(relay.at[h, c, three], relay_sem.at[h, c])
-        at_z, at_x = 2 * mz + mc, 2 * mx + mc
-        for i in (1, 3, 2):
+    def go_on(p):
+        h = lax.rem(p, 2)
+        wait(relay.at[p, three], relay_sem.at[p])
+        mine, other = turned(h, mz, mx)
+        slot = 2 * mine + mc
+        put(relay.at[p, four, 2 * mine + mate], recv.at[p, slot], pass_sem, recv_sem.at[p], mz, mx, mate)
+        for i in (2, 1, 3):
+            to = turn(mine, i)
+            z, x = turned(h, to, other)
             for d in range(2):
-                x, z = turn(mx, i), turn(mz, i)
-                put(relay.at[0, c, four, 2 * z + d], recv.at[0, c, at_z], pass_sem, recv_sem.at[0, c], z, mx, d)
-                put(relay.at[1, c, four, 2 * x + d], recv.at[1, c, at_x], pass_sem, recv_sem.at[1, c], mz, x, d)
-        put(relay.at[0, c, four, 2 * mz + mate], recv.at[0, c, at_z], pass_sem, recv_sem.at[0, c], mz, mx, mate)
-        put(relay.at[1, c, four, 2 * mx + mate], recv.at[1, c, at_x], pass_sem, recv_sem.at[1, c], mz, mx, mate)
-        recv[0, c, at_z] = relay[0, c, :, at_z]
-        recv[1, c, at_x] = relay[1, c, :, at_x]
+                put(relay.at[p, four, 2 * to + d], recv.at[p, slot], pass_sem, recv_sem.at[p], z, x, d)
+        recv[p, slot] = relay[p, :, slot]
+
+    def each(act, c):
+        def go(p, _):
+            act(p)
+            return 0
+
+        lax.fori_loop(2 * c, 2 * c + 2, go, 0)
+
+    def code_and_leave(p):
+        code(p)
+        leave(p)
 
     loads[0].wait()
+    lax.fori_loop(0, 4, add_up, 0)
+
+    each(code, 0)
+    pl.semaphore_wait(barrier, 16)
+    each(leave, 0)
     for copy in loads[2:]:
         copy.start()
-    lax.fori_loop(0, LOAD, add_up, 0)
-    code(0)
-    pl.semaphore_wait(barrier, 16)
-    leave(0)
     loads[1].wait()
-    lax.fori_loop(LOAD, 2 * LOAD, add_up, 0)
-    code(1)
-    leave(1)
-
-    for i in range(2, 12):
-        loads[i].wait()
-        lax.fori_loop(LOAD * i, LOAD * i + LOAD, add_up, 0)
+    lax.fori_loop(4, 8, add_up, 0)
+    each(code_and_leave, 1)
+    for copy, low, high in zip(loads[2:], (8, 16, 32), (16, 32, 48)):
+        copy.wait()
+        lax.fori_loop(low, high, add_up, 0)
 
     pad = jnp.zeros((16, 128), jnp.float32)
     for b in range(8):
@@ -205,13 +205,9 @@
         put(parts.at[mc, mz, mx], parts.at[mc, mz, mx], parts_send_sem.at[0], parts_recv_sem.at[0], mz, x, mc)
     sums_relay[mx] = sums_send[mx]
 
-    def code_and_leave(c, _):
-        code(c)
-        leave(c)
-        return 0
-
-    lax.fori_loop(2, AHEAD, code_and_leave, 0)
-    go_on(0)
+    for c in range(2, AHEAD):
+        each(code_and_leave, c)
+    each(go_on, 0)
 
     wait(sums_relay.at[three], sums_relay_sem)
     wait(parts.at[0, 0, three], parts_recv_sem.at[0])
@@ -224,9 +220,9 @@
     put(sums_relay.at[four, 2 * mz + mate], sums_recv.at[at_z], sums_pass_sem, sums_recv_sem, mz, mx, mate)
     sums_recv[at_z] = sums_relay[:, at_z]
 
-    code_and_leave(AHEAD, 0)
-    go_on(1)
-    code_and_leave(AHEAD + 1, 0)
+    each(code_and_leave, AHEAD)
+    each(go_on, 1)
+    each(code_and_leave, AHEAD + 1)
 
     wait(sums_recv.at[pl.ds(0, 7)], sums_recv_sem)
     wide = sums_recv[...].astype(jnp.float32).reshape(32, 16, 128)
@@ -238,15 +234,9 @@
 
     half = left_half()
 
-    def decode(c):
-        for h in range(2):
-            wait(recv.at[h, c, pl.ds(0, 7)], recv_sem.at[h, c])
-
-            def go(k, _):
-                decode_pair(recv, table, out, totals, wide_rows, c, h, k, (2 * c + h) * PER + k)
-                return 0
-
-            lax.fori_loop(0, PER, go, 0)
+    def decode(p):
+        wait(recv.at[p, pl.ds(0, 7)], recv_sem.at[p])
+        decode_pair(recv, table, out, totals, wide_rows, p, p)
 
     wait(parts.at[0, three], parts_recv_sem.at[1])
     put(parts.at[mc], parts.at[mc], parts_send_sem.at[2], parts_recv_sem.at[2], mz, mx, mate)
@@ -279,13 +269,13 @@
             ).start()
 
     def step(c, _):
-        go_on(c)
+        each(go_on, c)
 
         @pl.when(c < CHUNKS - AHEAD)
         def _():
-            code_and_leave(c + AHEAD, 0)
-
-        decode(c - 2)
+            each(code_and_leave, c + AHEAD)
+
+        each(decode, c - 2)
 
         @pl.when(c == CHUNKS // 2)
         def _():
@@ -294,7 +284,7 @@
         return 0
 
     lax.fori_loop(2, CHUNKS, step, 0)
-    decode(CHUNKS - 2)
+    each(decode, CHUNKS - 2)
     rest = pl.ds(0, 48)
     wait(router.at[rest], row_recv_sem)
     wait(router.at[rest], row_send_sem)
@@ -303,12 +293,11 @@
     wait(parts.at[0], parts_send_sem.at[2])
     wait(sums_send.at[three], sums_send_sem)
     wait(sums_recv.at[pl.ds(0, 7)], sums_pass_sem)
-    every = pl.ds(0, CHUNKS)
-    both = pl.ds(0, 2)
-    wait(send.at[both, every, three], send_sem)
-    for h in range(2):
-        wait(recv.at[h, CHUNKS - 1, pl.ds(0, 7)], recv_sem.at[h, CHUNKS - 1])
-    wait(recv.at[both, every, pl.ds(0, 7)], pass_sem)
+    every = pl.ds(0, PAIRS)
+    wait(send.at[every, three], send_sem)
+    for p in range(PAIRS - 2, PAIRS):
+        wait(recv.at[p, pl.ds(0, 7)], recv_sem.at[p])
+    wait(recv.at[every, pl.ds(0, 7)], pass_sem)
 
 
 def hand_out(
@@ -316,7 +305,7 @@
     gate, up, down, sg, su, sd, served,
     last, totals, scale, wide_rows, sem,
 ):
-    few = 4 * PER
+    few = 4
     copies = []
 
     def copy(src, dst):
@@ -328,17 +317,15 @@
         copy(out.at[pl.ds(16 * a, count)], big.at[pl.ds(0, count)])
     copy(router, served)
     totals[...] = begun[...]
-    for h in range(2):
-
-        def go(k, _):
-            decode_pair(recv, table, last, totals, wide_rows, CHUNKS - 1, h, k, h * PER + k)
-            return 0
-
-        lax.fori_loop(0, PER, go, 0)
-        part = 2 * PER
-        copy(last.at[pl.ds(part * h, part)], down.at[pl.ds(16 - few + part * h, part)])
-    turned = jnp.concatenate([totals[...], jnp.zeros((96, 128), jnp.float32)], axis=0).T
-    scale[...] = jnp.sqrt(turned[0:48, 0:32])
+
+    def go(i, _):
+        decode_pair(recv, table, last, totals, wide_rows, PAIRS - 2 + i, i)
+        return 0
+
+    lax.fori_loop(0, 2, go, 0)
+    copy(last, down.at[pl.ds(16 - few, few)])
+    across = jnp.concatenate([totals[...], jnp.zeros((96, 128), jnp.float32)], axis=0).T
+    scale[...] = jnp.sqrt(across[0:48, 0:32])
     for a, small in enumerate((sg, su, sd)):
         copy(scale.at[pl.ds(16 * a, 16)], small)
     for c in copies:
@@ -357,26 +344,26 @@
             pltpu.VMEM((48, 32, 2048), bf16),
             pltpu.VMEM((32, 128), f32),
             pltpu.VMEM((64, 2048), bf16),
-            pltpu.VMEM((2, CHUNKS, 8, 4, ROWS, 128), bf16),
+            pltpu.VMEM((PAIRS, 8, 4, 32, 128), bf16),
             pltpu.VMEM((64, 32, 128), f32),
         ),
         in_specs=[hbm, hbm, hbm, vmem, vmem],
         out_specs=(vmem,) * 5,
         scratch_shapes=[
             pltpu.VMEM((48, 64, 1024), f32),
-            pltpu.VMEM((2, CHUNKS, 4, 8, ROWS, 128), bf16),
-            pltpu.VMEM((2, CHUNKS, 4, 8, ROWS, 128), bf16),
+            pltpu.VMEM((PAIRS, 4, 8, 32, 128), bf16),
+            pltpu.VMEM((PAIRS, 4, 8, 32, 128), bf16),
             pltpu.VMEM((48, 1, 1024), f32),
             pltpu.VMEM((4, 8, 16, 128), bf16),
             pltpu.VMEM((4, 8, 16, 128), bf16),
             pltpu.VMEM((8, 4, 16, 128), bf16),
             pltpu.VMEM((2, 4, 4, 8, 128), bf16),
             pltpu.VMEM((2, 32, 2048), f32),
-            dma((12,)),
-            dma,
-            dma((2, CHUNKS)),
-            dma,
-            dma((2, CHUNKS)),
+            dma((5,)),
+            dma,
+            dma((PAIRS,)),
+            dma,
+            dma((PAIRS,)),
             dma,
             dma,
             dma,
@@ -399,11 +386,11 @@
         in_specs=[vmem] * 5,
         out_specs=(hbm,) * 7,
         scratch_shapes=[
-            pltpu.VMEM((4 * PER, 32, 2048), bf16),
+            pltpu.VMEM((4, 32, 2048), bf16),
             pltpu.VMEM((32, 128), f32),
             pltpu.VMEM((48, 32), f32),
             pltpu.VMEM((2, 32, 2048), f32),
-            dma((9,)),
+            dma((8,)),
         ],
         compiler_params=pltpu.CompilerParams(vmem_limit_bytes=16 * 2**20),
     )(*(pltpu.with_memory_space_constraint(a, pltpu.VMEM) for a in results))

time: 83.7 us -> 83 us (level)
  no operation moved by 1% of the time
where the time goes in v7:
time: 83 us; the launch traced here: 82.9 us
  Pallas kernels  82.2 us (99%)
    pallas_call x1, Pallas kernels, body(): pl.pallas_call(exchange, name='exchange', out_shape=(pltpu.VMEM((48, 32,...  79.4 us
    pallas_call x1, Pallas kernels, body(): pl.pallas_call(hand_out, name='hand_out', out_shape=(half, half, half, fe...  2.8 us

profile of v7, /device:TPU:1, one launch (start us, length us, event | category | flops | bytes accessed | tf_op | source)
XLA Modules:
  0.0 82.9 jit_solution(13406109550973762909)
XLA Ops:
  0.6 79.4 %exchange.1 = (bf16[48,32,2048]{2,1,0:T(8,128)(2,1)S(1)}, f32[32,128]{1,0:T(8,128)S(1)}, bf16[64,2048]{1,0:T(8,128)(2,1)S(1)}, bf16[24,8,4,32,128]{4,3,2,1,0:T(8,128)(2,1)S(1)}, f32[64,32,128]{2,1,0:T(8,128)S(1)}) custom-call(f32[16,64,1024]{2,1,0:T(8,128)} %gate.1, f32[16,64,1024]{2,1,0:T(8,128)} %up.1, f32[16,64,1024]{2,1,0:T(8,128)} %bitcast.6, ...), custom_call_target="tpu_custom_call" | custom-call | tf_op jit(solution)/shard_map/exchange/pallas_call | solution.py:340
  80.1 2.8 %hand_out.1 = (bf16[16,32,2048]{2,1,0:T(8,128)(2,1)}, bf16[16,32,2048]{2,1,0:T(8,128)(2,1)}, bf16[16,32,2048]{2,1,0:T(8,128)(2,1)}, f32[16,32]{1,0:T(8,128)}, f3...) custom-call(bf16[48,32,2048]{2,1,0:T(8,128)(2,1)S(1)} %get-tuple-element.19.out, ...), custom_call_target="tpu_custom_call" | custom-call | tf_op jit(solution)/shard_map/hand_out/pallas_call | solution.py:382

commit v8 on v7

--- a/solution.py
+++ b/solution.py
@@ -7,6 +7,8 @@
 
 MESH = pl.DeviceIdType.MESH
 CHUNKS = 12
+OWN, SHARED = 16, 16
+LAG = 4
 AHEAD = 4
 PAIRS = 24
 POWER = 20
@@ -60,10 +62,11 @@
 def exchange(
     gate, up, down, weight, gain,
     out, totals, router, recv, table,
-    xin, send, relay, sums, sums_send, sums_relay, sums_recv, parts, wide_rows,
+    xin, send, relay, squares, sums, sums_send, sums_relay, sums_recv, parts, wide_rows,
     in_sem, send_sem, relay_sem, pass_sem, recv_sem,
     sums_send_sem, sums_relay_sem, sums_pass_sem, sums_recv_sem,
     parts_send_sem, parts_recv_sem, row_send_sem, row_recv_sem,
+    mate_send_sem, mate_recv_sem,
 ):
     me = lax.axis_index("zero")
     bank = lax.axis_index("bank")
@@ -117,7 +120,15 @@
 
     def add_up(e, _):
         x = xin[e]
-        norm = jnp.sqrt(jnp.sum(x * x, axis=0, keepdims=True))
+        squares[0, e] = jnp.sum(x * x, axis=0, keepdims=True)
+        return 0
+
+    def own_norm(e, _):
+        sums[e] = jnp.sqrt(squares[0, e]).astype(jnp.bfloat16).astype(jnp.float32)
+        return 0
+
+    def chip_norm(e, _):
+        norm = jnp.sqrt(squares[0, e] + squares[1, e])
         sums[e] = norm.astype(jnp.bfloat16).astype(jnp.float32)
         return 0
 
@@ -179,7 +190,7 @@
 
     loads[0].wait()
     lax.fori_loop(0, 4, add_up, 0)
-
+    lax.fori_loop(0, 4, own_norm, 0)
     each(code, 0)
     pl.semaphore_wait(barrier, 16)
     each(leave, 0)
@@ -187,27 +198,47 @@
         copy.start()
     loads[1].wait()
     lax.fori_loop(4, 8, add_up, 0)
+    lax.fori_loop(4, 8, own_norm, 0)
     each(code_and_leave, 1)
-    for copy, low, high in zip(loads[2:], (8, 16, 32), (16, 32, 48)):
+    loads[2].wait()
+    lax.fori_loop(8, OWN, add_up, 0)
+    lax.fori_loop(8, OWN, own_norm, 0)
+    each(code_and_leave, 2)
+    each(code_and_leave, 3)
+
+    for copy, low, high in zip(loads[3:], (16, 32), (32, 48)):
         copy.wait()
         lax.fori_loop(low, high, add_up, 0)
-
-    pad = jnp.zeros((16, 128), jnp.float32)
+    rest = pl.ds(OWN, 48 - OWN)
+    put(squares.at[0, rest], squares.at[1, rest], mate_send_sem, mate_recv_sem, mz, mx, mate)
+    each(go_on, 0)
+    wait(squares.at[1, rest], mate_recv_sem)
+    lax.fori_loop(OWN, 48, chip_norm, 0)
+
     for b in range(8):
-        s = sums[:, 0, 128 * b : 128 * b + 128]
-        t = jnp.concatenate([s, pad, pltpu.roll(s, 112, 1), pad], axis=0).T
+        columns = slice(128 * b, 128 * b + 128)
+        s = jnp.concatenate(
+            [
+                sums[0:OWN, 0, columns],
+                sums[pl.ds(OWN + SHARED * mc, SHARED), 0, columns],
+            ],
+            axis=0,
+        )
+        t = jnp.concatenate(
+            [s] + [pltpu.roll(s, 128 - 8 * g, 1) for g in range(1, 4)], axis=0
+        ).T
         for q in range(4):
             z, x, d = b // 2, b % 2 * 2 + q // 2, q % 2
-            sums_send[x, 2 * z + d] = t[32 * q : 32 * q + 16].astype(jnp.bfloat16)
+            sums_send[x, 2 * z + d] = t[32 * q : 32 * q + 8].astype(jnp.bfloat16)
     for i in (1, 3, 2):
         x = turn(mx, i)
         put(sums_send.at[x], sums_relay.at[mx], sums_send_sem, sums_relay_sem, mz, x, mc)
         put(parts.at[mc, mz, mx], parts.at[mc, mz, mx], parts_send_sem.at[0], parts_recv_sem.at[0], mz, x, mc)
     sums_relay[mx] = sums_send[mx]
 
-    for c in range(2, AHEAD):
-        each(code_and_leave, c)
-    each(go_on, 0)
+    each(code_and_leave, AHEAD)
+    each(go_on, 1)
+    each(code_and_leave, AHEAD + 1)
 
     wait(sums_relay.at[three], sums_relay_sem)
     wait(parts.at[0, 0, three], parts_recv_sem.at[0])
@@ -220,16 +251,24 @@
     put(sums_relay.at[four, 2 * mz + mate], sums_recv.at[at_z], sums_pass_sem, sums_recv_sem, mz, mx, mate)
     sums_recv[at_z] = sums_relay[:, at_z]
 
-    each(code_and_leave, AHEAD)
-    each(go_on, 1)
-    each(code_and_leave, AHEAD + 1)
+    for c in range(2, LAG):
+        each(go_on, c)
+        each(code_and_leave, AHEAD + c)
 
     wait(sums_recv.at[pl.ds(0, 7)], sums_recv_sem)
-    wide = sums_recv[...].astype(jnp.float32).reshape(32, 16, 128)
-    for n in range(16):
+    wide = sums_recv[...].astype(jnp.float32).reshape(32, 8, 128)
+    core = lax.rem(lax.div(lax.broadcasted_iota(jnp.int32, (128, 128), 1), 4), 2)
+    for n in range(8):
         rows = jnp.concatenate([wide[:, n, :], jnp.zeros((96, 128), jnp.float32)], axis=0).T
-        table[:, n, :] = rows[0:64] * (1.0 / UP)
-        table[:, n + 16, :] = rows[64:128] * (1.0 / UP)
+        rows = rows * (1.0 / UP)
+        low = jnp.where(core == 0, rows, pltpu.roll(rows, 4, 1))
+        high = jnp.where(core == 1, rows, pltpu.roll(rows, 124, 1))
+        for g in range(4):
+            place = n + 8 * g
+            own, chip = 32 * g, 32 * g + OWN
+            table[0:OWN, place, :] = rows[own:chip]
+            table[OWN : OWN + SHARED, place, :] = low[chip : chip + SHARED]
+            table[OWN + SHARED : 48, place, :] = high[chip : chip + SHARED]
     totals[...] = jnp.zeros_like(totals)
 
     half = left_half()
@@ -275,7 +314,7 @@
         def _():
             each(code_and_leave, c + AHEAD)
 
-        each(decode, c - 2)
+        each(decode, c - LAG)
 
         @pl.when(c == CHUNKS // 2)
         def _():
@@ -283,11 +322,13 @@
 
         return 0
 
-    lax.fori_loop(2, CHUNKS, step, 0)
-    each(decode, CHUNKS - 2)
-    rest = pl.ds(0, 48)
-    wait(router.at[rest], row_recv_sem)
-    wait(router.at[rest], row_send_sem)
+    lax.fori_loop(LAG, CHUNKS, step, 0)
+    for c in range(CHUNKS - LAG, CHUNKS - 1):
+        each(decode, c)
+    columns = pl.ds(0, 48)
+    wait(router.at[columns], row_recv_sem)
+    wait(router.at[columns], row_send_sem)
+    wait(squares.at[1, rest], mate_send_sem)
     wait(parts.at[0, 0, three], parts_send_sem.at[0])
     wait(parts.at[0, three], parts_send_sem.at[1])
     wait(parts.at[0], parts_send_sem.at[2])
@@ -345,7 +386,7 @@
             pltpu.VMEM((32, 128), f32),
             pltpu.VMEM((64, 2048), bf16),
             pltpu.VMEM((PAIRS, 8, 4, 32, 128), bf16),
-            pltpu.VMEM((64, 32, 128), f32),
+            pltpu.VMEM((48, 32, 128), f32),
         ),
         in_specs=[hbm, hbm, hbm, vmem, vmem],
         out_specs=(vmem,) * 5,
@@ -353,10 +394,11 @@
             pltpu.VMEM((48, 64, 1024), f32),
             pltpu.VMEM((PAIRS, 4, 8, 32, 128), bf16),
             pltpu.VMEM((PAIRS, 4, 8, 32, 128), bf16),
+            pltpu.VMEM((2, 48, 1, 1024), f32),
             pltpu.VMEM((48, 1, 1024), f32),
-            pltpu.VMEM((4, 8, 16, 128), bf16),
-            pltpu.VMEM((4, 8, 16, 128), bf16),
-            pltpu.VMEM((8, 4, 16, 128), bf16),
+            pltpu.VMEM((4, 8, 8, 128), bf16),
+            pltpu.VMEM((4, 8, 8, 128), bf16),
+            pltpu.VMEM((8, 4, 8, 128), bf16),
             pltpu.VMEM((2, 4, 4, 8, 128), bf16),
             pltpu.VMEM((2, 32, 2048), f32),
             dma((5,)),
@@ -370,6 +412,8 @@
             dma,
             dma((3,)),
             dma((3,)),
+            dma,
+            dma,
             dma,
             dma,
         ],

time: 83 us -> 82.2 us (level)
    pallas_call x1, Pallas kernels: 79.4 us -> 78.6 us  [body(): pl.pallas_call(exchange, name='exchange', out_shape=(pltpu.VMEM((48, 32,...]
where the time goes in v8:
time: 82.2 us; the launch traced here: 82 us
  Pallas kernels  81.4 us (99%)
    pallas_call x1, Pallas kernels, body(): pl.pallas_call(exchange, name='exchange', out_shape=(pltpu.VMEM((48, 32,...  78.6 us
    pallas_call x1, Pallas kernels, body(): pl.pallas_call(hand_out, name='hand_out', out_shape=(half, half, half, fe...  2.8 us

profile of v8, /device:TPU:1, one launch (start us, length us, event | category | flops | bytes accessed | tf_op | source)
XLA Modules:
  0.0 82.0 jit_solution(6202498414441323991)
XLA Ops:
  0.6 78.6 %exchange.1 = (bf16[48,32,2048]{2,1,0:T(8,128)(2,1)S(1)}, f32[32,128]{1,0:T(8,128)S(1)}, bf16[64,2048]{1,0:T(8,128)(2,1)S(1)}, bf16[24,8,4,32,128]{4,3,2,1,0:T(8,128)(2,1)S(1)}, f32[48,32,128]{2,1,0:T(8,128)S(1)}) custom-call(f32[16,64,1024]{2,1,0:T(8,128)} %gate.1, f32[16,64,1024]{2,1,0:T(8,128)} %up.1, f32[16,64,1024]{2,1,0:T(8,128)} %bitcast.6, ...), custom_call_target="tpu_custom_call" | custom-call | tf_op jit(solution)/shard_map/exchange/pallas_call | solution.py:381
  79.2 2.8 %hand_out.1 = (bf16[16,32,2048]{2,1,0:T(8,128)(2,1)}, bf16[16,32,2048]{2,1,0:T(8,128)(2,1)}, bf16[16,32,2048]{2,1,0:T(8,128)(2,1)}, f32[16,32]{1,0:T(8,128)}, f3...) custom-call(bf16[48,32,2048]{2,1,0:T(8,128)(2,1)S(1)} %get-tuple-element.19.out, ...), custom_call_target="tpu_custom_call" | custom-call | tf_op jit(solution)/shard_map/hand_out/pallas_call | solution.py:426

commit v9 on v8

--- a/solution.py
+++ b/solution.py
@@ -9,7 +9,7 @@
 CHUNKS = 12
 OWN, SHARED = 16, 16
 LAG = 4
-AHEAD = 4
+AHEAD = 6
 PAIRS = 24
 POWER = 20
 UP = 2.0**6.25
@@ -92,6 +92,20 @@
     def wait(ref, sem):
         pltpu.make_async_copy(ref, ref, sem).wait()
 
+    barrier = pltpu.get_barrier_semaphore()
+
+    def greet(**where):
+        pl.semaphore_signal(
+            barrier, inc=1, device_id=where, device_id_type=MESH
+        )
+
+    for i in (2, 1, 3):
+        for c in range(2):
+            greet(zero=device(turn(mz, i), mx, c))
+            greet(zero=device(mz, turn(mx, i), c))
+        greet(bank=turn(bank, i))
+    greet(zero=device(mz, mx, mate))
+
     loads = [
         pltpu.make_async_copy(
             ref.at[pl.ds(k, count)], xin.at[pl.ds(16 * a + k, count)], in_sem.at[i]
@@ -101,20 +115,6 @@
     for copy in loads[:2]:
         copy.start()
 
-    barrier = pltpu.get_barrier_semaphore()
-
-    def greet(**where):
-        pl.semaphore_signal(
-            barrier, inc=1, device_id=where, device_id_type=MESH
-        )
-
-    greet(zero=device(mz, mx, mate))
-    for i in (1, 3, 2):
-        for c in range(2):
-            greet(zero=device(turn(mz, i), mx, c))
-            greet(zero=device(mz, turn(mx, i), c))
-        greet(bank=turn(bank, i))
-
     part = (weight[...] * gain[...]).astype(jnp.bfloat16)
     parts[mc, mz, mx] = jnp.concatenate([part[0:8], part[8:16]], axis=1)
 
@@ -124,7 +124,9 @@
         return 0
 
     def own_norm(e, _):
-        sums[e] = jnp.sqrt(squares[0, e]).astype(jnp.bfloat16).astype(jnp.float32)
+        x = xin[e]
+        norm = jnp.sqrt(jnp.sum(x * x, axis=0, keepdims=True))
+        sums[e] = norm.astype(jnp.bfloat16).astype(jnp.float32)
         return 0
 
     def chip_norm(e, _):
@@ -189,7 +191,6 @@
         leave(p)
 
     loads[0].wait()
-    lax.fori_loop(0, 4, add_up, 0)
     lax.fori_loop(0, 4, own_norm, 0)
     each(code, 0)
     pl.semaphore_wait(barrier, 16)
@@ -197,11 +198,9 @@
     for copy in loads[2:]:
         copy.start()
     loads[1].wait()
-    lax.fori_loop(4, 8, add_up, 0)
     lax.fori_loop(4, 8, own_norm, 0)
     each(code_and_leave, 1)
     loads[2].wait()
-    lax.fori_loop(8, OWN, add_up, 0)
     lax.fori_loop(8, OWN, own_norm, 0)
     each(code_and_leave, 2)
     each(code_and_leave, 3)
@@ -236,7 +235,8 @@
         put(parts.at[mc, mz, mx], parts.at[mc, mz, mx], parts_send_sem.at[0], parts_recv_sem.at[0], mz, x, mc)
     sums_relay[mx] = sums_send[mx]
 
-    each(code_and_leave, AHEAD)
+    for c in range(4, AHEAD + 1):
+        each(code_and_leave, c)
     each(go_on, 1)
     each(code_and_leave, AHEAD + 1)
 

time: 82.2 us -> 82.2 us (level)
  no operation moved by 1% of the time
where the time goes in v9:
time: 82.2 us; the launch traced here: 82 us
  Pallas kernels  81.4 us (99%)
    pallas_call x1, Pallas kernels, body(): pl.pallas_call(exchange, name='exchange', out_shape=(pltpu.VMEM((48, 32,...  78.6 us
    pallas_call x1, Pallas kernels, body(): pl.pallas_call(hand_out, name='hand_out', out_shape=(half, half, half, fe...  2.8 us

profile of v9, /device:TPU:1, one launch (start us, length us, event | category | flops | bytes accessed | tf_op | source)
XLA Modules:
  0.0 82.0 jit_solution(14413994986608490330)
XLA Ops:
  0.6 78.6 %exchange.1 = (bf16[48,32,2048]{2,1,0:T(8,128)(2,1)S(1)}, f32[32,128]{1,0:T(8,128)S(1)}, bf16[64,2048]{1,0:T(8,128)(2,1)S(1)}, bf16[24,8,4,32,128]{4,3,2,1,0:T(8,128)(2,1)S(1)}, f32[48,32,128]{2,1,0:T(8,128)S(1)}) custom-call(f32[16,64,1024]{2,1,0:T(8,128)} %gate.1, f32[16,64,1024]{2,1,0:T(8,128)} %up.1, f32[16,64,1024]{2,1,0:T(8,128)} %bitcast.6, ...), custom_call_target="tpu_custom_call" | custom-call | tf_op jit(solution)/shard_map/exchange/pallas_call | solution.py:381
  79.2 2.8 %hand_out.1 = (bf16[16,32,2048]{2,1,0:T(8,128)(2,1)}, bf16[16,32,2048]{2,1,0:T(8,128)(2,1)}, bf16[16,32,2048]{2,1,0:T(8,128)(2,1)}, f32[16,32]{1,0:T(8,128)}, f3...) custom-call(bf16[48,32,2048]{2,1,0:T(8,128)(2,1)S(1)} %get-tuple-element.19.out, ...), custom_call_target="tpu_custom_call" | custom-call | tf_op jit(solution)/shard_map/hand_out/pallas_call | solution.py:426

commit v10 on v8

--- a/solution.py
+++ b/solution.py
@@ -116,7 +116,8 @@
         greet(bank=turn(bank, i))
 
     part = (weight[...] * gain[...]).astype(jnp.bfloat16)
-    parts[mc, mz, mx] = jnp.concatenate([part[0:8], part[8:16]], axis=1)
+    row, spot = turned(mc, mz, mx)
+    parts[mc, row, spot] = jnp.concatenate([part[0:8], part[8:16]], axis=1)
 
     def add_up(e, _):
         x = xin[e]
@@ -233,7 +234,8 @@
     for i in (1, 3, 2):
         x = turn(mx, i)
         put(sums_send.at[x], sums_relay.at[mx], sums_send_sem, sums_relay_sem, mz, x, mc)
-        put(parts.at[mc, mz, mx], parts.at[mc, mz, mx], parts_send_sem.at[0], parts_recv_sem.at[0], mz, x, mc)
+        z_to, x_to = turned(mc, row, turn(spot, i))
+        put(parts.at[mc, row, spot], parts.at[mc, row, spot], parts_send_sem.at[0], parts_recv_sem.at[0], z_to, x_to, mc)
     sums_relay[mx] = sums_send[mx]
 
     each(code_and_leave, AHEAD)
@@ -247,7 +249,8 @@
         z = turn(mz, i)
         for d in range(2):
             put(sums_relay.at[four, 2 * z + d], sums_recv.at[at_z], sums_pass_sem, sums_recv_sem, z, mx, d)
-        put(parts.at[mc, mz], parts.at[mc, mz], parts_send_sem.at[1], parts_recv_sem.at[1], z, mx, mc)
+        z_to, x_to = turned(mc, turn(row, i), spot)
+        put(parts.at[mc, row], parts.at[mc, row], parts_send_sem.at[1], parts_recv_sem.at[1], z_to, x_to, mc)
     put(sums_relay.at[four, 2 * mz + mate], sums_recv.at[at_z], sums_pass_sem, sums_recv_sem, mz, mx, mate)
     sums_recv[at_z] = sums_relay[:, at_z]
 
@@ -288,7 +291,7 @@
         for t in range(16):
             z, x = t // 4, t % 4
             a = parts[0, z, x].astype(jnp.float32)
-            b = parts[1, z, x].astype(jnp.float32)
+            b = parts[1, x, z].astype(jnp.float32)
             block = jnp.concatenate(
                 [
                     jnp.where(low, a, pltpu.roll(b, 64, 1)),

time: 82.2 us -> 82.1 us (level)
  no operation moved by 1% of the time
where the time goes in v10:
time: 82.1 us; the launch traced here: 81.9 us
  Pallas kernels  81.3 us (99%)
    pallas_call x1, Pallas kernels, body(): pl.pallas_call(exchange, name='exchange', out_shape=(pltpu.VMEM((48, 32,...  78.5 us
    pallas_call x1, Pallas kernels, body(): pl.pallas_call(hand_out, name='hand_out', out_shape=(half, half, half, fe...  2.8 us

profile of v10, /device:TPU:1, one launch (start us, length us, event | category | flops | bytes accessed | tf_op | source)
XLA Modules:
  0.0 81.9 jit_solution(282138758176908862)
XLA Ops:
  0.6 78.5 %exchange.1 = (bf16[48,32,2048]{2,1,0:T(8,128)(2,1)S(1)}, f32[32,128]{1,0:T(8,128)S(1)}, bf16[64,2048]{1,0:T(8,128)(2,1)S(1)}, bf16[24,8,4,32,128]{4,3,2,1,0:T(8,128)(2,1)S(1)}, f32[48,32,128]{2,1,0:T(8,128)S(1)}) custom-call(f32[16,64,1024]{2,1,0:T(8,128)} %gate.1, f32[16,64,1024]{2,1,0:T(8,128)} %up.1, f32[16,64,1024]{2,1,0:T(8,128)} %bitcast.6, ...), custom_call_target="tpu_custom_call" | custom-call | tf_op jit(solution)/shard_map/exchange/pallas_call | solution.py:384
  79.1 2.8 %hand_out.1 = (bf16[16,32,2048]{2,1,0:T(8,128)(2,1)}, bf16[16,32,2048]{2,1,0:T(8,128)(2,1)}, bf16[16,32,2048]{2,1,0:T(8,128)(2,1)}, f32[16,32]{1,0:T(8,128)}, f3...) custom-call(bf16[48,32,2048]{2,1,0:T(8,128)(2,1)S(1)} %get-tuple-element.19.out, ...), custom_call_target="tpu_custom_call" | custom-call | tf_op jit(solution)/shard_map/hand_out/pallas_call | solution.py:429

commit v11 on v9

--- a/solution.py
+++ b/solution.py
@@ -116,7 +116,8 @@
         copy.start()
 
     part = (weight[...] * gain[...]).astype(jnp.bfloat16)
-    parts[mc, mz, mx] = jnp.concatenate([part[0:8], part[8:16]], axis=1)
+    row, spot = turned(mc, mz, mx)
+    parts[mc, row, spot] = jnp.concatenate([part[0:8], part[8:16]], axis=1)
 
     def add_up(e, _):
         x = xin[e]
@@ -232,7 +233,8 @@
     for i in (1, 3, 2):
         x = turn(mx, i)
         put(sums_send.at[x], sums_relay.at[mx], sums_send_sem, sums_relay_sem, mz, x, mc)
-        put(parts.at[mc, mz, mx], parts.at[mc, mz, mx], parts_send_sem.at[0], parts_recv_sem.at[0], mz, x, mc)
+        z_to, x_to = turned(mc, row, turn(spot, i))
+        put(parts.at[mc, row, spot], parts.at[mc, row, spot], parts_send_sem.at[0], parts_recv_sem.at[0], z_to, x_to, mc)
     sums_relay[mx] = sums_send[mx]
 
     for c in range(4, AHEAD + 1):
@@ -247,7 +249,8 @@
         z = turn(mz, i)
         for d in range(2):
             put(sums_relay.at[four, 2 * z + d], sums_recv.at[at_z], sums_pass_sem, sums_recv_sem, z, mx, d)
-        put(parts.at[mc, mz], parts.at[mc, mz], parts_send_sem.at[1], parts_recv_sem.at[1], z, mx, mc)
+        z_to, x_to = turned(mc, turn(row, i), spot)
+        put(parts.at[mc, row], parts.at[mc, row], parts_send_sem.at[1], parts_recv_sem.at[1], z_to, x_to, mc)
     put(sums_relay.at[four, 2 * mz + mate], sums_recv.at[at_z], sums_pass_sem, sums_recv_sem, mz, mx, mate)
     sums_recv[at_z] = sums_relay[:, at_z]
 
@@ -288,7 +291,7 @@
         for t in range(16):
             z, x = t // 4, t % 4
             a = parts[0, z, x].astype(jnp.float32)
-            b = parts[1, z, x].astype(jnp.float32)
+            b = parts[1, x, z].astype(jnp.float32)
             block = jnp.concatenate(
                 [
                     jnp.where(low, a, pltpu.roll(b, 64, 1)),

time: 82.2 us -> 82.1 us (level)
  no operation moved by 1% of the time
where the time goes in v11:
time: 82.1 us; the launch traced here: 81.9 us
  Pallas kernels  81.3 us (99%)
    pallas_call x1, Pallas kernels, body(): pl.pallas_call(exchange, name='exchange', out_shape=(pltpu.VMEM((48, 32,...  78.5 us
    pallas_call x1, Pallas kernels, body(): pl.pallas_call(hand_out, name='hand_out', out_shape=(half, half, half, fe...  2.8 us

profile of v11, /device:TPU:1, one launch (start us, length us, event | category | flops | bytes accessed | tf_op | source)
XLA Modules:
  0.0 81.9 jit_solution(15917592331550883509)
XLA Ops:
  0.6 78.5 %exchange.1 = (bf16[48,32,2048]{2,1,0:T(8,128)(2,1)S(1)}, f32[32,128]{1,0:T(8,128)S(1)}, bf16[64,2048]{1,0:T(8,128)(2,1)S(1)}, bf16[24,8,4,32,128]{4,3,2,1,0:T(8,128)(2,1)S(1)}, f32[48,32,128]{2,1,0:T(8,128)S(1)}) custom-call(f32[16,64,1024]{2,1,0:T(8,128)} %gate.1, f32[16,64,1024]{2,1,0:T(8,128)} %up.1, f32[16,64,1024]{2,1,0:T(8,128)} %bitcast.6, ...), custom_call_target="tpu_custom_call" | custom-call | tf_op jit(solution)/shard_map/exchange/pallas_call | solution.py:384
  79.1 2.8 %hand_out.1 = (bf16[16,32,2048]{2,1,0:T(8,128)(2,1)}, bf16[16,32,2048]{2,1,0:T(8,128)(2,1)}, bf16[16,32,2048]{2,1,0:T(8,128)(2,1)}, f32[16,32]{1,0:T(8,128)}, f3...) custom-call(bf16[48,32,2048]{2,1,0:T(8,128)(2,1)S(1)} %get-tuple-element.19.out, ...), custom_call_target="tpu_custom_call" | custom-call | tf_op jit(solution)/shard_map/hand_out/pallas_call | solution.py:429
